TPU v7x, 64 devices: a 2x2x8 block of a 4x4x8 slice. The times are simulated.
64 devices in a mesh: dp: 4 (over x, y), dpa: 16 (over z, core).
Axes of the slice: x: 2, y: 2, z: 8, core: 2. Of those that a mesh axis runs over, the one named last changes fastest.
The devices are a block of a 4x4x8 slice.
Arguments:
- x: bfloat16 [64, 1, 384, 2048], P(('dp', 'dpa')), parts along dimension 0
- chunk_len: int32 [64, 1], P(('dp', 'dpa')), parts along dimension 0
- ctx_len: int32 [64, 1], P(('dp', 'dpa')), parts along dimension 0
- lat_cache: bfloat16 [64, 1, 1024, 512], P(('dp', 'dpa')), parts along dimension 0
- rope_cache: bfloat16 [64, 1, 1024, 64], P(('dp', 'dpa')), parts along dimension 0
- topk_idx: int32 [64, 1, 384, 6], P(('dp', 'dpa')), parts along dimension 0
- g_attn: bfloat16 [2048], replicated
- w_q: bfloat16 [2048, 16, 192], replicated
- w_dkv: bfloat16 [2048, 512], replicated
- g_kv: bfloat16 [512], replicated
- w_kr: bfloat16 [2048, 64], replicated
- w_uk: bfloat16 [512, 16, 128], replicated
- w_uv: bfloat16 [512, 16, 128], replicated
- w_o: bfloat16 [16, 128, 2048], replicated
- g_ffn: bfloat16 [2048], replicated
- w_router: bfloat16 [2048, 64], replicated
- w_sh_gate: bfloat16 [2048, 2816], replicated
- w_sh_up: bfloat16 [2048, 2816], replicated
- w_sh_down: bfloat16 [2816, 2048], replicated
- w_exp_gate: bfloat16 [64, 2048, 1408], P('dpa')
- w_exp_up: bfloat16 [64, 2048, 1408], P('dpa')
- w_exp_down: bfloat16 [64, 1408, 2048], P('dpa')
Outputs:
- output 1: bfloat16 [64, 1, 384, 2048], P(('dp', 'dpa')), parts along dimension 0
- output 2: bfloat16 [64, 1, 1024, 512], P(('dp', 'dpa')), parts along dimension 0
- output 3: bfloat16 [64, 1, 1024, 64], P(('dp', 'dpa')), parts along dimension 0
There are 4 independent parts. A program takes and returns all parts, laid end to end along the dimension named above; an argument that names none is the same for every part.
All inputs are finite; a program needn't handle non-finite values.
Results may differ from a plain program's by a relative error of at most 0.0196086.
Values are sent between devices in bfloat16 or wider.
A program may use at most 768 MiB of HBM per device.

v0:
```python
import jax
import jax.numpy as jnp
from jax import lax
from jax.sharding import PartitionSpec as P

EPS = 1e-6
THETA = 10000.0


def rms_norm(vals, gain):
    vals_f32 = vals.astype(jnp.float32)
    inv_rms = lax.rsqrt(jnp.mean(vals_f32 * vals_f32, axis=-1, keepdims=True) + EPS)
    return (vals_f32 * inv_rms * gain.astype(jnp.float32)).astype(jnp.bfloat16)


def rope_tables(positions, half):
    inv_freq = THETA ** (-2.0 * jnp.arange(half, dtype=jnp.float32) / (2 * half))
    angle = positions.astype(jnp.float32)[..., None] * inv_freq
    return jnp.cos(angle), jnp.sin(angle)


def rotate(vals, cos_tab, sin_tab):
    half = cos_tab.shape[-1]
    first = vals[..., :half]
    second = vals[..., half:]
    return jnp.concatenate([first * cos_tab - second * sin_tab, second * cos_tab + first * sin_tab], axis=-1)


def write_window(cache_row, new_rows, start, keep):
    old_rows = lax.dynamic_slice_in_dim(cache_row, start, new_rows.shape[0], axis=0)
    merged = jnp.where(keep[:, None], new_rows, old_rows)
    return lax.dynamic_update_slice_in_dim(cache_row, merged, start, axis=0)


def attention_block(x_in, chunk_len, ctx_len, lat_cache, rope_cache, g_attn, w_q, w_dkv, g_kv, w_kr, w_uk, w_uv, w_o):
    chunk = x_in.shape[2]
    ctx_max = lat_cache.shape[2]
    rope_dim = w_kr.shape[1]
    nope_dim = w_q.shape[2] - rope_dim
    scale = w_q.shape[2] ** -0.5
    normed = rms_norm(x_in, g_attn)
    q_full = jnp.einsum('brcd,dhq->brchq', normed, w_q, preferred_element_type=jnp.float32).astype(jnp.bfloat16)
    positions = ctx_len[:, :, None] + jnp.arange(chunk)
    cos_tab, sin_tab = rope_tables(positions, rope_dim // 2)
    q_rope = rotate(q_full[..., nope_dim:].astype(jnp.float32), cos_tab[..., None, :], sin_tab[..., None, :]).astype(jnp.bfloat16)
    q_lat = jnp.einsum('brchn,khn->brchk', q_full[..., :nope_dim], w_uk, preferred_element_type=jnp.float32).astype(jnp.bfloat16)
    lat_new = rms_norm(jnp.einsum('brcd,dk->brck', normed, w_dkv, preferred_element_type=jnp.float32), g_kv)
    rope_new = rotate(jnp.einsum('brcd,dp->brcp', normed, w_kr, preferred_element_type=jnp.float32), cos_tab, sin_tab).astype(jnp.bfloat16)
    keep = jnp.arange(chunk) < chunk_len[:, :, None]
    writer = jax.vmap(jax.vmap(write_window))
    lat_upd = writer(lat_cache, lat_new, ctx_len, keep)
    rope_upd = writer(rope_cache, rope_new, ctx_len, keep)
    key_pos = jnp.arange(ctx_max)

    def one_request(index):
        q_lat_req = lax.dynamic_index_in_dim(q_lat, index, axis=1, keepdims=False)
        q_rope_req = lax.dynamic_index_in_dim(q_rope, index, axis=1, keepdims=False)
        lat_req = lax.dynamic_index_in_dim(lat_upd, index, axis=1, keepdims=False)
        rope_req = lax.dynamic_index_in_dim(rope_upd, index, axis=1, keepdims=False)
        pos_req = lax.dynamic_index_in_dim(positions, index, axis=1, keepdims=False)
        scores = (jnp.einsum('bchk,blk->bchl', q_lat_req, lat_req, preferred_element_type=jnp.float32) + jnp.einsum('bchp,blp->bchl', q_rope_req, rope_req, preferred_element_type=jnp.float32)) * scale
        visible = key_pos[None, None, None, :] <= pos_req[:, :, None, None]
        scores = jnp.where(visible, scores, -1e30)
        attn_prob = jax.nn.softmax(scores, axis=-1).astype(jnp.bfloat16)
        return jnp.einsum('bchl,blk->bchk', attn_prob, lat_req, preferred_element_type=jnp.float32).astype(jnp.bfloat16)

    out_lat = lax.map(one_request, jnp.arange(x_in.shape[1]))
    out_head = jnp.einsum('rbchk,khv->brchv', out_lat, w_uv, preferred_element_type=jnp.float32).astype(jnp.bfloat16)
    attn_out = jnp.einsum('brchv,hvd->brcd', out_head, w_o, preferred_element_type=jnp.float32).astype(jnp.bfloat16)
    hidden = (x_in.astype(jnp.float32) + attn_out.astype(jnp.float32)).astype(jnp.bfloat16)
    return hidden, lat_upd, rope_upd


def router_and_shared(hidden_rows, g_ffn, w_router, w_sh_gate, w_sh_up, w_sh_down):
    normed = rms_norm(hidden_rows, g_ffn)
    route_prob = jax.nn.softmax(jnp.dot(normed, w_router, preferred_element_type=jnp.float32), axis=-1)
    shared_act = (jax.nn.silu(jnp.dot(normed, w_sh_gate, preferred_element_type=jnp.float32)) * jnp.dot(normed, w_sh_up, preferred_element_type=jnp.float32)).astype(jnp.bfloat16)
    shared_out = jnp.dot(shared_act, w_sh_down, preferred_element_type=jnp.float32)
    return normed, route_prob, shared_out


def expert_ffn(sorted_rows, sizes, w_exp_gate, w_exp_up, w_exp_down):
    gate_part = lax.ragged_dot(sorted_rows, w_exp_gate, sizes, preferred_element_type=jnp.float32)
    up_part = lax.ragged_dot(sorted_rows, w_exp_up, sizes, preferred_element_type=jnp.float32)
    act = (jax.nn.silu(gate_part) * up_part).astype(jnp.bfloat16)
    return lax.ragged_dot(act, w_exp_down, sizes, preferred_element_type=jnp.float32).astype(jnp.bfloat16)


def solution(mesh):
    group = mesh.shape['dpa']
    tok_spec = P(('dp', 'dpa'))
    whole = P()
    exp_spec = P('dpa')

    def device_step(x_in, chunk_len, ctx_len, lat_cache, rope_cache, topk_idx, g_attn, w_q, w_dkv, g_kv, w_kr, w_uk, w_uv, w_o, g_ffn, w_router, w_sh_gate, w_sh_up, w_sh_down, w_exp_gate, w_exp_up, w_exp_down):
        hidden, lat_upd, rope_upd = attention_block(x_in, chunk_len, ctx_len, lat_cache, rope_cache, g_attn, w_q, w_dkv, g_kv, w_kr, w_uk, w_uv, w_o)
        chunk = hidden.shape[2]
        width = hidden.shape[3]
        tokens = hidden.shape[1] * chunk
        top_k = topk_idx.shape[-1]
        local_exp = w_exp_gate.shape[0]
        capacity = tokens * top_k // group
        flat_h = hidden.reshape(tokens, width)
        normed, route_prob, shared_out = router_and_shared(flat_h, g_ffn, w_router, w_sh_gate, w_sh_up, w_sh_down)
        valid = (jnp.arange(chunk)[None, :] < chunk_len[0][:, None]).reshape(tokens)
        choice = topk_idx.reshape(tokens, top_k)
        gates = jnp.take_along_axis(route_prob, choice, axis=1)
        flat_choice = choice.reshape(tokens * top_k)
        target = flat_choice // local_exp
        hits = (target[:, None] == jnp.arange(group)[None, :]).astype(jnp.int32)
        rank_in = jnp.sum(jnp.cumsum(hits, axis=0) * hits, axis=1) - 1
        slot = target * capacity + rank_in
        pair_of_slot = jnp.argsort(slot)
        pair_valid = jnp.repeat(valid, top_k)
        expert_key = jnp.where(pair_valid, flat_choice % local_exp, local_exp).astype(jnp.int32)
        send_rows = normed[pair_of_slot // top_k]
        send_key = expert_key[pair_of_slot]
        recv_rows = lax.all_to_all(send_rows, 'dpa', 0, 0, tiled=True)
        recv_key = lax.all_to_all(send_key, 'dpa', 0, 0, tiled=True)
        order = jnp.argsort(recv_key, stable=True)
        sizes = jnp.bincount(recv_key, length=local_exp + 1)[:local_exp].astype(jnp.int32)
        sorted_out = expert_ffn(recv_rows[order], sizes, w_exp_gate, w_exp_up, w_exp_down)
        expert_rows = sorted_out[jnp.argsort(order)]
        back_rows = lax.all_to_all(expert_rows, 'dpa', 0, 0, tiled=True)
        pair_out = back_rows[slot].reshape(tokens, top_k, width)
        routed = jnp.sum(gates[:, :, None] * pair_out.astype(jnp.float32), axis=1)
        total = flat_h.astype(jnp.float32) + shared_out + routed
        result = jnp.where(valid[:, None], total, 0.0).astype(jnp.bfloat16)
        return result.reshape(hidden.shape), lat_upd, rope_upd

    return jax.shard_map(device_step, mesh=mesh, in_specs=(tok_spec,) * 6 + (whole,) * 13 + (exp_spec,) * 3, out_specs=(tok_spec, tok_spec, tok_spec), check_vma=False)
```

profile of v0, /device:TPU:21, one launch (start us, length us, event | category | flops | bytes accessed | tf_op | source)
XLA Modules:
  0.0 854.0 jit_solution(6027928083031944752)
XLA Ops:
  26.0 12.3 %gather_fusion.1 = s32[2304]{0:T(1024)S(1)} fusion(s32[2304]{0:T(1024)S(1)} %get-tuple-element.99, s32[3072]{0:T(1024)S(1)} %get-tuple-element.113), kind=kCustom, calls=%fused_computation.1 | custom fusion | bytes 27648 | tf_op jit(solution)/shard_map/gather | solution.py:117
  39.0 11.4 %all-to-all-start.1 = ((s32[16,144,1]{1,2,0:T(1,128)}), s32[16,144,1]{1,2,0:T(1,128)S(1)}, u32[]{:S(2)}, u32[]{:S(2)}) async-start(s32[16,144,1]{1,2,0:T(1,128)} %all_to_all.33), calls=%async_computation.1 | async-start | bytes 32768 | tf_op jit(solution)/shard_map/all_to_all | solution.py:119
  52.2 10.0 %fusion.86 = f32[384,3072]{0,1:S(1)} fusion(bf16[2048,3072]{0,1:T(8,128)(2,1)} %bitcast.146, bf16[1,1,384,2048]{3,2,1,0:T(8,128)(2,1)} %param.26, f32[2048]{0:T(1024)S(1)} %convert_element_type.134, f32[384]{0:T(512)S(1)} %add_rsqrt_fusion.2), kind=kOutput, calls=%fused_computation.155 | convolution fusion | flops 4834983936 | bytes 18884096
  86.3 14.4 %fusion.2 = f32[384,16,1024]{2,0,1:T(8,128)} fusion(bf16[512,16,128]{2,1,0:T(8,128)(2,1)S(1)} %copy-done, bf16[1,1,384,16,192]{2,4,3,1,0:T(8,128)(2,1)} %convert_bitcast_fusion, bf16[1,1,1024,512]{3,2,1,0:T(8,128)(2,1)S(1)} %scatter.6), kind=kOutput, calls=%fused_computation.14 | convolution fusion | flops 7250903040 | bytes 29884416 | tf_op jit(solution)/shard_map/while/body/eval_jaxpr/bchk,blk->bchl/dot_general | solution.py:61
  102.4 18.4 %fusion.90 = f32[384,16]{0,1:T(8,128)S(1)} fusion(f32[384,16,1024]{2,0,1:T(8,128)} %fusion.2, pred[384,1024]{1,0:T(8,128)(4,1)} %iota_compare_fusion, bf16[384,16,32]{0,2,1:T(8,128)(2,1)S(1)} %get-tuple-element.94, bf16[384,16,32]{0,2,1:T(8,128)(2,1)S(1)} %get-tuple-element.93, bf16[1,1,1024,64]{2,3,1,0:T(8,128)(2,1)S(1)} %scatter.9), kind=kOutput, calls=%fused_computation.158 | convolution fusion | flops 838337536 | bytes 26501120 | tf_op jit(solution)/shard_map/while/body/eval_jaxpr/sub | solution.py:64
  120.8 15.5 %multiply_select_fusion = f32[384,16,1024]{2,0,1:T(8,128)} fusion(f32[384,16,1024]{2,0,1:T(8,128)} %fusion.2, pred[384,1024]{1,0:T(8,128)(4,1)S(1)} %copy-done.6, bf16[384,16,32]{0,2,1:T(8,128)(2,1)S(1)} %get-tuple-element.94, bf16[384,16,32]{0,2,1:T(8,128)(2,1)S(1)} %get-tuple-element.93, bf16[1,1,1024,64]{2,3,1,0:T(8,128)(2,1)S(1)} %scatter.9), kind=kOutput, calls=%fused_computation.11 | convolution fusion | flops 825753600 | bytes 51642368 | tf_op jit(solution)/shard_map/while/body/eval_jaxpr/bchp,blp->bchl/dot_general | solution.py:61
  136.3 25.0 %fusion.26 = bf16[16,384,128]{2,1,0:T(8,128)(2,1)} fusion(bf16[512,16,128]{2,1,0:T(8,128)(2,1)} %param.38, f32[384,16]{0,1:T(8,128)S(1)} %fusion.90, bf16[1,1,1024,512]{3,2,1,0:T(8,128)(2,1)S(1)} %scatter.6, f32[384,16,1024]{2,0,1:T(8,128)} %multiply_select_fusion), kind=kOutput, calls=%fused_computation.45 | convolution fusion | flops 7270571008 | bytes 29908992 | tf_op jit(solution)/shard_map/rbchk,khv->brchv/dot_general | solution.py:68
  169.7 9.9 %gather_fusion = bf16[2304,2048]{1,0:T(8,128)(2,1)} fusion(bf16[384,2048]{1,0:T(8,128)(2,1)S(1)} %fusion.16, s32[3072]{0:T(1024)S(1)} %get-tuple-element.112), kind=kCustom, calls=%fused_computation | custom fusion | bytes 18883584 | tf_op jit(solution)/shard_map/gather | solution.py:116
  187.2 17.0 %scatter_custom_fusion = s32[5]{0:T(128)} fusion(s32[2304]{0:T(1024)S(1)} %reshape.852, s32[2304]{0:T(1024)S(1)} %ne.62, s32[]{:T(128)} %constant.174.clone.1), kind=kCustom, calls=%fused_computation.147 | custom fusion | flops 2304 | bytes 24 | tf_op jit(solution)/shard_map/scatter-add | solution.py:121
  217.3 182.4 %all-to-all-done = bf16[16,144,2048]{2,1,0:T(8,128)(2,1)} async-done(((bf16[16,144,2048]{2,1,0:T(8,128)(2,1)}), bf16[16,144,2048]{2,1,0:T(8,128)(2,1)}, u32[]{:S(2)}, u32[]{:S(2)}) %all-to-all-start) | async-done | bytes 9437216 | tf_op jit(solution)/shard_map/all_to_all | solution.py:118
  399.7 23.2 %gather_fusion.2 = bf16[2304,2048]{1,0:T(8,128)(2,1)} fusion(bf16[2304,2048]{1,0:T(8,128)(2,1)} %bitcast.38, s32[3072]{0:T(1024)S(1)} %pad_clamp_fusion.2), kind=kCustom, calls=%fused_computation.2 | custom fusion | bytes 18883584 | tf_op jit(solution)/shard_map/gather | solution.py:122
  422.9 28.6 %ragged-dot-none.1 = f32[2304,1408]{1,0:T(8,128)} custom-call(s32[1]{0:T(128)} %get-tuple-element.79, s32[5]{0:T(128)} %get-tuple-element.80, s32[12]{0:T(128)} %get-tuple-element.81, s32[12]{0:T(128)} %get-tuple-element.82, s32[1]{0:T(128)} %get-tuple-element.79, bf16[2304,2048]{1,0:T(8,128)(2,1)} %gather_fusion.2, bf16[4,2048,1408]{2,1,0:T(8,128)(2,1)} %param.46), custom_call_target="tpu_custom_call" | custom-call | flops 13287555072 | bytes 45482000 | tf_op jit(solution)/shard_map/ragged_dot_general/ragged-dot-none
  451.6 28.4 %ragged-dot-none.2 = f32[2304,1408]{1,0:T(8,128)} custom-call(s32[1]{0:T(128)} %get-tuple-element.79, s32[5]{0:T(128)} %get-tuple-element.80, s32[12]{0:T(128)} %get-tuple-element.81, s32[12]{0:T(128)} %get-tuple-element.82, s32[1]{0:T(128)} %get-tuple-element.79, bf16[2304,2048]{1,0:T(8,128)(2,1)} %gather_fusion.2, bf16[4,2048,1408]{2,1,0:T(8,128)(2,1)} %param.45), custom_call_target="tpu_custom_call" | custom-call | flops 13287555072 | bytes 45482000 | tf_op jit(solution)/shard_map/ragged_dot_general/ragged-dot-none
  480.0 12.6 %multiply_convert_fusion = bf16[2304,1408]{1,0:T(8,128)(2,1)} fusion(f32[2304,1408]{1,0:T(8,128)} %ragged-dot-none.1, f32[2304,1408]{1,0:T(8,128)} %ragged-dot-none.2), kind=kLoop, calls=%fused_computation.12 | loop fusion | flops 19464192 | bytes 32440320 | tf_op jit(solution)/shard_map/convert_element_type | solution.py:85
  492.6 29.2 %ragged-dot-none = f32[2304,2048]{1,0:T(8,128)} custom-call(s32[1]{0:T(128)} %get-tuple-element.79, s32[5]{0:T(128)} %get-tuple-element.80, s32[12]{0:T(128)} %get-tuple-element.81, s32[12]{0:T(128)} %get-tuple-element.82, s32[1]{0:T(128)} %get-tuple-element.79, bf16[2304,1408]{1,0:T(8,128)(2,1)} %multiply_convert_fusion, bf16[4,1408,2048]{2,1,0:T(8,128)(2,1)} %param.47), custom_call_target="tpu_custom_call" | custom-call | flops 13287555072 | bytes 48431120 | tf_op jit(solution)/shard_map/ragged_dot_general/ragged-dot-none
  521.8 11.4 %convert_element_type.163 = bf16[2304,2048]{1,0:T(8,128)(2,1)} convert(f32[2304,2048]{1,0:T(8,128)} %ragged-dot-none) | non-fusion elementwise | flops 4718592 | bytes 28311552 | tf_op jit(solution)/shard_map/convert_element_type | solution.py:86
  533.2 23.3 %gather_fusion.3 = bf16[2304,2048]{1,0:T(8,128)(2,1)} fusion(bf16[2304,2048]{1,0:T(8,128)(2,1)} %convert_element_type.163, s32[3072]{0:T(1024)S(1)} %pad_clamp_fusion.1), kind=kCustom, calls=%fused_computation.3 | custom fusion | bytes 18883584 | tf_op jit(solution)/shard_map/gather | solution.py:123
  566.3 18.0 %gather_fusion.5 = f32[2304]{0:T(1024)S(1)} fusion(f32[384,64]{0,1:T(8,128)S(1)} %fusion.52, s32[2304]{0:T(1024)S(1)} %reshape.844), kind=kCustom, calls=%fused_computation.5 | custom fusion | bytes 36864 | tf_op jit(solution)/shard_map/jit(take_along_axis)/gather | solution.py:107
  584.6 9.6 %fusion.96 = f32[384,2816]{1,0:T(8,128)} fusion(bf16[384,2048]{1,0:T(8,128)(2,1)S(1)} %fusion.16, bf16[2048,2816]{1,0:T(8,128)(2,1)} %param.42), kind=kOutput, calls=%fused_computation.160 | convolution fusion | flops 4429185024 | bytes 17432576 | tf_op jit(solution)/shard_map/dot_general | solution.py:77
  594.2 183.4 %all-to-all-done.2 = bf16[16,144,2048]{2,1,0:T(8,128)(2,1)} async-done(((bf16[16,144,2048]{2,1,0:T(8,128)(2,1)}), bf16[16,144,2048]{2,1,0:T(8,128)(2,1)}, u32[]{:S(2)}, u32[]{:S(2)}) %all-to-all-start.2) | async-done | bytes 9437216 | tf_op jit(solution)/shard_map/all_to_all | solution.py:124
  777.5 23.2 %gather_fusion.4 = bf16[2304,2048]{1,0:T(8,128)(2,1)} fusion(bf16[2304,2048]{1,0:T(8,128)(2,1)} %bitcast.40, s32[3072]{0:T(1024)S(1)} %pad_clamp_fusion), kind=kCustom, calls=%fused_computation.4 | custom fusion | bytes 18883584 | tf_op jit(solution)/shard_map/gather | solution.py:125
  800.7 16.9 %reshape.801 = f32[384,6,2048]{2,1,0:T(8,128)} reshape(bf16[2304,2048]{1,0:T(8,128)(2,1)} %gather_fusion.4) | data formatting | bytes 28311552 | tf_op jit(solution)/shard_map/convert_element_type | solution.py:126
  817.6 15.0 %multiply_reduce_fusion = f32[384,2048]{1,0:T(8,128)} fusion(f32[384,6,2048]{2,1,0:T(8,128)} %reshape.801, f32[384,6]{1,0:T(8,128)S(1)} %and_select_fusion), kind=kLoop, calls=%fused_computation.8 | loop fusion | flops 8650752 | bytes 22029312 | tf_op jit(solution)/shard_map/reduce_sum | solution.py:126
  832.7 21.2 %fusion.21 = bf16[1,1,384,2048]{3,2,1,0:T(8,128)(2,1)} fusion(f32[384,2048]{1,0:T(8,128)} %multiply_reduce_fusion, bf16[2816,2048]{1,0:T(8,128)(2,1)} %param.44, bf16[384,2048]{1,0:T(8,128)(2,1)} %copy-done.9, pred[384]{0:T(512)(128)(4,1)S(1)} %copy-done.16, bf16[384,2048]{1,0:T(8,128)(2,1)} %copy-done.2, bf16[2048,2816]{1,0:T(8,128)(2,1)} %param.43, ...), kind=kOutput, calls=%fused_computation.40 | convolution fusion | flops 8868790272 | bytes 35258752 | tf_op jit(solution)/shard_map/dot_general | solution.py:78
  (123 shorter events, 91.0 us)
Async XLA Ops:
  0.6 85.7 %copy-start = (bf16[512,16,128]{2,1,0:T(8,128)(2,1)S(1)}, bf16[512,16,128]{2,1,0:T(8,128)(2,1)}, u32[]{:S(2)}) copy-start(bf16[512,16,128]{2,1,0:T(8,128)(2,1)} %param.37) | copy-start | bytes 6291460
  4.4 14.2 %copy-start.3 = (s32[1,1,384,6]{3,2,1,0:T(8,128)}, s32[1,1,384,6]{3,2,1,0:T(8,128)S(1)}, u32[]{:S(2)}) copy-start(s32[1,1,384,6]{3,2,1,0:T(8,128)S(1)} %copy.40) | copy-start | bytes 27652
  18.3 64.9 %copy-start.15 = (pred[384]{0:T(512)(128)(4,1)}, pred[384]{0:T(512)(128)(4,1)S(1)}, u32[]{:S(2)}) copy-start(pred[384]{0:T(512)(128)(4,1)S(1)} %iota_compare_fusion.3) | copy-start | bytes 1156
  26.0 24.4 %copy-start.17 = (bf16[2048]{0:T(1024)(128)(2,1)S(1)}, bf16[2048]{0:T(1024)(128)(2,1)}, u32[]{:S(2)}) copy-start(bf16[2048]{0:T(1024)(128)(2,1)} %param.32) | copy-start | bytes 12292
  39.0 140.5 %all-to-all-start.1 = ((s32[16,144,1]{1,2,0:T(1,128)}), s32[16,144,1]{1,2,0:T(1,128)S(1)}, u32[]{:S(2)}, u32[]{:S(2)}) async-start(s32[16,144,1]{1,2,0:T(1,128)} %all_to_all.33), calls=%async_computation.1 | async-start | bytes 32768 | tf_op jit(solution)/shard_map/all_to_all | solution.py:119
  62.3 2.9 copy-start.22
  65.2 2.4 copy-start.21
  65.2 3.1 copy-start.19
  65.2 3.1 copy-start.20
  77.0 59.3 %copy-start.5 = (bf16[1,1,1024,512]{3,2,1,0:T(8,128)(2,1)}, bf16[1,1,1024,512]{3,2,1,0:T(8,128)(2,1)S(1)}, u32[]{:S(2)}) copy-start(bf16[1,1,1024,512]{3,2,1,0:T(8,128)(2,1)S(1)} %scatter.6) | copy-start | bytes 3145732
  77.0 6.2 copy-start.10
  86.3 34.4 %copy-start.11 = (bf16[1,1,1024,64]{2,3,1,0:T(8,128)(2,1)}, bf16[1,1,1024,64]{2,3,1,0:T(8,128)(2,1)S(1)}, u32[]{:S(2)}) copy-start(bf16[1,1,1024,64]{2,3,1,0:T(8,128)(2,1)S(1)} %scatter.9) | copy-start | bytes 393220
  102.3 18.4 %copy-start.6 = (pred[384,1024]{1,0:T(8,128)(4,1)S(1)}, pred[384,1024]{1,0:T(8,128)(4,1)}, u32[]{:S(2)}) copy-start(pred[384,1024]{1,0:T(8,128)(4,1)} %iota_compare_fusion) | copy-start | bytes 1179652
  120.8 15.6 %copy-start.18 = (bf16[2048]{0:T(1024)(128)(2,1)S(1)}, bf16[2048]{0:T(1024)(128)(2,1)}, u32[]{:S(2)}) copy-start(bf16[2048]{0:T(1024)(128)(2,1)} %param.40) | copy-start | bytes 12292
  136.3 25.0 %copy-start.8 = (bf16[1,1,384,2048]{3,2,1,0:T(8,128)(2,1)S(1)}, bf16[1,1,384,2048]{3,2,1,0:T(8,128)(2,1)}, u32[]{:S(2)}) copy-start(bf16[1,1,384,2048]{3,2,1,0:T(8,128)(2,1)} %param.26) | copy-start | bytes 4718596
  169.6 415.0 %copy-start.2 = (bf16[384,2048]{1,0:T(8,128)(2,1)}, bf16[384,2048]{1,0:T(8,128)(2,1)S(1)}, u32[]{:S(2)}) copy-start(bf16[384,2048]{1,0:T(8,128)(2,1)S(1)} %fusion.16) | copy-start | bytes 4718596
  179.5 220.2 %all-to-all-start = ((bf16[16,144,2048]{2,1,0:T(8,128)(2,1)}), bf16[16,144,2048]{2,1,0:T(8,128)(2,1)}, u32[]{:S(2)}, u32[]{:S(2)}) async-start(bf16[16,144,2048]{2,1,0:T(8,128)(2,1)} %bitcast.141), calls=%async_computation | async-start | bytes 18874368 | tf_op jit(solution)/shard_map/all_to_all | solution.py:118
  556.5 8.6 %copy-start.4 = (s32[1,1,384,6]{3,2,1,0:T(8,128)S(1)}, s32[1,1,384,6]{3,2,1,0:T(8,128)}, u32[]{:S(2)}) copy-start(s32[1,1,384,6]{3,2,1,0:T(8,128)} %copy-done.3) | copy-start | bytes 27652
  556.5 8.7 %copy-start.14 = (s32[1,1,384,6]{2,1,3,0:T(1,128)S(1)}, s32[1,1,384,6]{2,1,3,0:T(1,128)}, u32[]{:S(2)}) copy-start(s32[1,1,384,6]{2,1,3,0:T(1,128)} %param.31) | copy-start | bytes 27652
  556.5 9.1 %copy-start.12 = (bf16[2048,64]{0,1:T(8,128)(2,1)S(1)}, bf16[2048,64]{0,1:T(8,128)(2,1)}, u32[]{:S(2)}) copy-start(bf16[2048,64]{0,1:T(8,128)(2,1)} %param.41) | copy-start | bytes 786436
  556.5 221.0 %all-to-all-start.2 = ((bf16[16,144,2048]{2,1,0:T(8,128)(2,1)}), bf16[16,144,2048]{2,1,0:T(8,128)(2,1)}, u32[]{:S(2)}, u32[]{:S(2)}) async-start(bf16[16,144,2048]{2,1,0:T(8,128)(2,1)} %bitcast.142), calls=%async_computation.2 | async-start | bytes 18874368 | tf_op jit(solution)/shard_map/all_to_all | solution.py:124
  566.3 18.2 %copy-start.13 = (s32[2304]{0:T(1024)S(1)}, s32[2304]{0:T(1024)}, u32[]{:S(2)}) copy-start(s32[2304]{0:T(1024)} %get-tuple-element.97) | copy-start | bytes 27652
  817.6 15.0 %copy-start.16 = (pred[384]{0:T(512)(128)(4,1)S(1)}, pred[384]{0:T(512)(128)(4,1)}, u32[]{:S(2)}) copy-start(pred[384]{0:T(512)(128)(4,1)} %copy-done.15) | copy-start | bytes 1156
  832.7 21.2 %copy-start.1 = (bf16[512,16,128]{2,1,0:T(8,128)(2,1)S(1)}, bf16[512,16,128]{2,1,0:T(8,128)(2,1)}, u32[]{:S(2)}) copy-start(bf16[512,16,128]{2,1,0:T(8,128)(2,1)} %param.37) | copy-start | bytes 6291460
  (2 other events, 3.0 us)
where the time goes:
time: 859 us; the launch traced here: 854 us
  waiting for transfers between devices  366 us (43%)
  local copies, waits for them, and re-layouts  142 us (17%)
  matrix products  125 us (15%)
  other arithmetic  104 us (12%)
  Pallas kernels  87.7 us (10%)
  starting transfers between devices  27.4 us (3%)
    all_to_all x1, waiting for transfers between devices, device_step(): back_rows = lax.all_to_all(expert_rows, 'dpa', 0, 0, tiled=True)  183 us
    all_to_all x1, waiting for transfers between devices, device_step(): recv_rows = lax.all_to_all(send_rows, 'dpa', 0, 0, tiled=True)  182 us
    another operation x3, Pallas kernels  86.3 us
    dot_general x1, matrix products, attention_block(): jnp.einsum('rbchk,khv->brchv', out_lat, w_uv, preferred_element_type=jnp....  25 us
    gather x1, local copies, waits for them, and re-layouts, device_step(): expert_rows = sorted_out[jnp.argsort(order)]  23.3 us
    gather x1, local copies, waits for them, and re-layouts, device_step(): pair_out = back_rows[slot].reshape(tokens, top_k, width)  23.2 us
    gather x1, local copies, waits for them, and re-layouts, device_step(): recv_rows[order]  23.2 us
    dot_general x1, matrix products, router_and_shared(): jnp.dot(shared_act, w_sh_down, preferred_element_type=jnp.float32)  21.2 us
  transfers between devices with their start and end apart: 3, of which 2 were waited for; matrix products, arithmetic and copies ran while one was open for 22% of the time, Pallas kernels for 0%

commit v1 on v0

--- a/solution.py
+++ b/solution.py
@@ -1,6 +1,10 @@
+import functools
+
 import jax
 import jax.numpy as jnp
 from jax import lax
+from jax.experimental import pallas as pl
+from jax.experimental.pallas import tpu as pltpu
 from jax.sharding import PartitionSpec as P
 
 EPS = 1e-6
@@ -71,19 +75,398 @@
     return hidden, lat_upd, rope_upd
 
 
-def router_and_shared(hidden_rows, g_ffn, w_router, w_sh_gate, w_sh_up, w_sh_down):
-    normed = rms_norm(hidden_rows, g_ffn)
-    route_prob = jax.nn.softmax(jnp.dot(normed, w_router, preferred_element_type=jnp.float32), axis=-1)
-    shared_act = (jax.nn.silu(jnp.dot(normed, w_sh_gate, preferred_element_type=jnp.float32)) * jnp.dot(normed, w_sh_up, preferred_element_type=jnp.float32)).astype(jnp.bfloat16)
-    shared_out = jnp.dot(shared_act, w_sh_down, preferred_element_type=jnp.float32)
-    return normed, route_prob, shared_out
-
-
-def expert_ffn(sorted_rows, sizes, w_exp_gate, w_exp_up, w_exp_down):
-    gate_part = lax.ragged_dot(sorted_rows, w_exp_gate, sizes, preferred_element_type=jnp.float32)
-    up_part = lax.ragged_dot(sorted_rows, w_exp_up, sizes, preferred_element_type=jnp.float32)
-    act = (jax.nn.silu(gate_part) * up_part).astype(jnp.bfloat16)
-    return lax.ragged_dot(act, w_exp_down, sizes, preferred_element_type=jnp.float32).astype(jnp.bfloat16)
+MESH_ID = pl.DeviceIdType.MESH
+F32 = jnp.float32
+BF16 = jnp.bfloat16
+LANES = 128
+SUB = 8
+
+
+def moe_kernel(dims, u_ref, h_ref, tk_ref, len_ref, wr_ref, wsg, wsu, wsd, wg, wu, wd, y_ref, rows_all, back, tk_all, slot_in, slot_out, gates, sh_act, picked, act, sent, row_exp, acc, w_gu, w_dn, stage, three, tk_s, tk_r, ring_s, ring_r, sib_s, sib_r, own_s, own_r, back_s, back_r, gu_sem, dn_sem, st_sem, th_sem, loc_sem):
+    group, tokens, width, cap, local, ff, shared_ff, top_k, experts = dims
+    ring = group // 2
+    half = tokens // 2
+    chunk_rows = 4 * cap
+    gu_tiles = local * ff // LANES
+    per_exp = ff // LANES
+    sh_tiles = shared_ff // LANES
+    dn_cols = w_dn.shape[2]
+    dn_tiles = width // dn_cols
+    me = lax.axis_index('dpa')
+    zpos = lax.div(me, 2)
+    core = lax.rem(me, 2)
+
+    def dev(zz, cc):
+        return lax.rem(zz + 2 * ring, ring) * 2 + cc
+
+    def remote(src, dst, s_sem, r_sem, to):
+        return pltpu.make_async_remote_copy(src_ref=src, dst_ref=dst, send_sem=s_sem, recv_sem=r_sem, device_id={'dpa': to}, device_id_type=MESH_ID)
+
+    barrier = pltpu.get_barrier_semaphore()
+
+    def greet(i, carry):
+        pl.semaphore_signal(barrier, inc=1, device_id={'dpa': lax.rem(me + i, group)}, device_id_type=MESH_ID)
+        return carry
+
+    lax.fori_loop(1, group, greet, 0)
+    pl.semaphore_wait(barrier, group - 1)
+
+    def tk_copy(i, owner):
+        return remote(tk_ref, tk_all.at[owner], tk_s.at[i], tk_r.at[i], lax.rem(me + i, group))
+
+    def tk_start(i, carry):
+        tk_copy(i, me).start()
+        return carry
+
+    lax.fori_loop(1, group, tk_start, 0)
+
+    def ring_copy(way, hop, part, sending):
+        sign = 1 - 2 * way
+        owner = dev(zpos - sign * (hop - 1 if sending else hop), core)
+        rows = pl.ds(part * half, half)
+        dst = rows_all.at[owner, rows]
+        src = u_ref.at[rows] if sending and hop == 1 else dst
+        return remote(src, dst, ring_s.at[way, hop - 1, part], ring_r.at[way, hop - 1, part], dev(zpos + sign, core))
+
+    def sib_copy(way, hop, part, cc):
+        sign = 1 - 2 * way
+        block = rows_all.at[dev(zpos - sign * hop, cc), pl.ds(part * half, half)]
+        return remote(block, block, sib_s.at[way, hop - 1, part], sib_r.at[way, hop - 1, part], dev(zpos, 1 - core))
+
+    far = ring // 2
+
+    def in_ring(way, hop, part):
+        return hop < far or (hop == far and part == way)
+
+    def own_copy(cc):
+        return remote(u_ref, rows_all.at[dev(zpos, cc)], own_s, own_r, dev(zpos, 1 - core))
+
+    keep_own = pltpu.make_async_copy(u_ref, rows_all.at[me], loc_sem.at[0])
+    for part in range(2):
+        for way in range(2):
+            ring_copy(way, 1, part, True).start()
+    own_copy(core).start()
+    keep_own.start()
+
+    def relay(hop, part):
+        for way in range(2):
+            if in_ring(way, hop, part):
+                ring_copy(way, hop, part, False).wait_recv()
+                if in_ring(way, hop + 1, part):
+                    ring_copy(way, hop + 1, part, True).start()
+                sib_copy(way, hop, part, core).start()
+
+    def gu_copies(shared, t):
+        slot = lax.rem(t, w_gu.shape[0])
+        if shared:
+            cols = pl.ds(pl.multiple_of(t * LANES, LANES), LANES)
+            srcs = (wsg.at[:, cols], wsu.at[:, cols])
+        else:
+            cols = pl.ds(pl.multiple_of(lax.rem(t, per_exp) * LANES, LANES), LANES)
+            exp = lax.div(t, per_exp)
+            srcs = (wg.at[exp, :, cols], wu.at[exp, :, cols])
+        return [pltpu.make_async_copy(src, w_gu.at[slot, :, pl.ds(i * LANES, LANES)], gu_sem.at[slot, i]) for i, src in enumerate(srcs)]
+
+    def dn_copy(shared, t):
+        slot = lax.rem(t, w_dn.shape[0])
+        cols = pl.ds(pl.multiple_of(t * dn_cols, dn_cols), dn_cols)
+        if shared:
+            return pltpu.make_async_copy(wsd.at[:, cols], w_dn.at[slot, pl.ds(0, shared_ff)], dn_sem.at[slot])
+        return pltpu.make_async_copy(wd.at[:, cols], w_dn.at[slot], dn_sem.at[slot])
+
+    gu_ahead = w_gu.shape[0] - 1
+    dn_ahead = w_dn.shape[0] - 1
+
+    def gu_start(shared, t):
+        for copy in gu_copies(shared, t):
+            copy.start()
+
+    def prime_gu(shared):
+        for t in range(gu_ahead):
+            gu_start(shared, jnp.int32(t))
+
+    def prime_dn(shared):
+        for t in range(dn_ahead):
+            dn_copy(shared, jnp.int32(t)).start()
+
+    prime_gu(True)
+    prime_dn(True)
+
+    logits = lax.dot_general(wr_ref[...], u_ref[...], (((1,), (1,)), ((), ())), preferred_element_type=F32)
+    shifted = jnp.exp(logits - jnp.max(logits, axis=0, keepdims=True))
+    prob = shifted / jnp.sum(shifted, axis=0, keepdims=True)
+    exp_row = lax.broadcasted_iota(jnp.int32, (experts, tokens), 0)
+    for k in range(SUB):
+        if k < top_k:
+            gates[k:k + 1, :] = jnp.sum(jnp.where(exp_row == tk_ref[k:k + 1, :], prob, 0.0), axis=0, keepdims=True)
+        else:
+            gates[k:k + 1, :] = jnp.zeros((1, tokens), F32)
+
+    def glu(both):
+        gate = both[:, :LANES]
+        return gate * jax.nn.sigmoid(gate) * both[:, LANES:]
+
+    def sh_gu(t, carry):
+        @pl.when(t + gu_ahead < sh_tiles)
+        def _():
+            gu_start(True, t + gu_ahead)
+
+        for copy in gu_copies(True, t):
+            copy.wait()
+        both = jnp.dot(u_ref[...], w_gu[lax.rem(t, w_gu.shape[0])], preferred_element_type=F32)
+        sh_act[:, pl.ds(pl.multiple_of(t * LANES, LANES), LANES)] = glu(both).astype(BF16)
+        return carry
+
+    lax.fori_loop(0, sh_tiles, sh_gu, 0)
+    prime_gu(False)
+    relay(1, 0)
+
+    def sh_dn(t, carry):
+        @pl.when(t + dn_ahead < dn_tiles)
+        def _():
+            dn_copy(True, t + dn_ahead).start()
+
+        dn_copy(True, t).wait()
+        cols = pl.ds(pl.multiple_of(t * dn_cols, dn_cols), dn_cols)
+        tile = w_dn[lax.rem(t, w_dn.shape[0]), :shared_ff]
+        acc[:, cols] = h_ref[:, cols].astype(F32) + jnp.dot(sh_act[...], tile, preferred_element_type=F32)
+        return carry
+
+    lax.fori_loop(0, dn_tiles, sh_dn, 0)
+    prime_dn(False)
+
+    tk_all[me] = tk_ref[...]
+
+    def tk_wait(i, carry):
+        tk_copy(i, lax.rem(me - i + group, group)).wait_recv()
+        return carry
+
+    lax.fori_loop(1, group, tk_wait, 0)
+    rows8 = group * SUB
+    before = (lax.broadcasted_iota(jnp.int32, (tokens, tokens), 0) < lax.broadcasted_iota(jnp.int32, (tokens, tokens), 1)).astype(F32).astype(BF16)
+    row_a = lax.broadcasted_iota(jnp.int32, (rows8, rows8), 0)
+    row_b = lax.broadcasted_iota(jnp.int32, (rows8, rows8), 1)
+    above = jnp.logical_and(row_b < row_a, lax.div(row_b, SUB) == lax.div(row_a, SUB)).astype(F32).astype(BF16)
+    row_id = lax.broadcasted_iota(jnp.int32, (rows8, tokens), 0)
+    is_choice = lax.rem(row_id, SUB) < top_k
+
+    def slots(hit):
+        ones = hit.astype(F32).astype(BF16)
+        upto = jnp.dot(ones, before, preferred_element_type=F32)
+        rows_up = jnp.sum(jnp.dot(above, ones, preferred_element_type=F32), axis=1, keepdims=True)
+        return upto + rows_up
+
+    all_tk = tk_all[...].reshape(rows8, tokens)
+    hit_in = jnp.logical_and(is_choice, lax.div(all_tk, local) == me)
+    own_len = jnp.broadcast_to(tk_all[:, top_k:top_k + 1, :], (group, SUB, tokens)).reshape(rows8, tokens)
+    live = jnp.logical_and(hit_in, lax.broadcasted_iota(jnp.int32, (rows8, tokens), 1) < own_len)
+    slot_in[...] = jnp.where(live, slots(hit_in), -1.0).reshape(group, SUB, tokens)
+    own_tk = jnp.broadcast_to(tk_ref[...][None], (group, SUB, tokens)).reshape(rows8, tokens)
+    hit_out = jnp.logical_and(is_choice, lax.div(own_tk, local) == lax.div(row_id, SUB))
+    slot_out[...] = jnp.where(hit_out, slots(hit_out), -1.0).reshape(group, SUB, tokens)
+
+    keep_own.wait()
+    relay(1, 1)
+
+    slot_row = lax.broadcasted_iota(jnp.int32, (cap, tokens), 0).astype(F32)
+
+    def source(c, j):
+        side = lax.div(j, 2)
+        zz = zpos + (1 - side) * (c + 1) - side * lax.rem(c + 1, far)
+        return dev(zz, lax.rem(j, 2))
+
+    def send_back(c, j, to):
+        block = sent.at[c, pl.ds(pl.multiple_of(j * cap, 16), cap)]
+        return remote(block, back.at[me], back_s.at[c * 4 + j], back_r.at[c * 4 + lax.div(j, 2) * 2 + core], to)
+
+    def chunk(c, carry):
+        for hop in range(1, far + 1):
+            @pl.when(c == hop - 1)
+            def _():
+                for part in range(2):
+                    for way in range(2):
+                        if in_ring(way, hop, part):
+                            sib_copy(way, hop, part, 1 - core).wait_recv()
+                if hop == far:
+                    own_copy(1 - core).wait_recv()
+
+        def load(j):
+            slot = lax.rem(j, 2)
+            return pltpu.make_async_copy(rows_all.at[source(c, j)], stage.at[slot], st_sem.at[slot])
+
+        load(jnp.int32(0)).start()
+
+        def gather(j, inner):
+            @pl.when(j < 3)
+            def _():
+                load(j + 1).start()
+
+            src = source(c, j)
+            pick = jnp.zeros((cap, tokens), F32)
+            which = jnp.zeros((cap, tokens), F32)
+            for k in range(top_k):
+                same = slot_row == slot_in[src, k:k + 1, :]
+                pick = jnp.where(same, 1.0, pick)
+                which = jnp.where(same, lax.rem(tk_all[src, k:k + 1, :], local).astype(F32), which)
+            rows = pl.ds(pl.multiple_of(j * cap, 16), cap)
+            row_exp[rows, :] = jnp.broadcast_to(jnp.sum(which, axis=1, keepdims=True), (cap, LANES))
+            load(j).wait()
+            picked[rows, :] = jnp.dot(pick.astype(BF16), stage[lax.rem(j, 2)], preferred_element_type=F32).astype(BF16)
+            return inner
+
+        lax.fori_loop(0, 4, gather, 0)
+
+        @pl.when(c > 0)
+        def _():
+            for j in range(4):
+                send_back(c - 1, j, source(c - 1, jnp.int32(j))).start()
+
+        def gate_up(t, inner):
+            @pl.when(t + gu_ahead < gu_tiles)
+            def _():
+                gu_start(False, t + gu_ahead)
+
+            for copy in gu_copies(False, t):
+                copy.wait()
+            for when_c, when_t, hop, part in EVENTS:
+                @pl.when(jnp.logical_and(c == when_c, t == when_t * gu_tiles // 44))
+                def _():
+                    relay(hop, part)
+
+            both = jnp.dot(picked[...], w_gu[lax.rem(t, w_gu.shape[0])], preferred_element_type=F32)
+            mine = row_exp[...] == lax.div(t, per_exp).astype(F32)
+            act[:, pl.ds(pl.multiple_of(t * LANES, LANES), LANES)] = jnp.where(mine, glu(both), 0.0).astype(BF16)
+            return inner
+
+        lax.fori_loop(0, gu_tiles, gate_up, 0)
+
+        @pl.when(c < 3)
+        def _():
+            prime_gu(False)
+
+        def down(t, inner):
+            @pl.when(t + dn_ahead < dn_tiles)
+            def _():
+                dn_copy(False, t + dn_ahead).start()
+
+            dn_copy(False, t).wait()
+            out = jnp.dot(act[...], w_dn[lax.rem(t, w_dn.shape[0])], preferred_element_type=F32)
+            sent[c, :, pl.ds(pl.multiple_of(t * dn_cols, dn_cols), dn_cols)] = out.astype(BF16)
+            return inner
+
+        lax.fori_loop(0, dn_tiles, down, 0)
+
+        @pl.when(c < 3)
+        def _():
+            prime_dn(False)
+
+        return carry
+
+    lax.fori_loop(0, 4, chunk, 0)
+    for j in range(2):
+        send_back(jnp.int32(3), jnp.int32(j), source(jnp.int32(3), jnp.int32(j))).start()
+    send_back(jnp.int32(3), 3 - core, dev(zpos, 1 - core)).start()
+    mine = pltpu.make_async_copy(sent.at[3, pl.ds(pl.multiple_of((2 + core) * cap, 16), cap)], back.at[me], back_r.at[14 + core])
+    mine.start()
+
+    def combine(i, carry):
+        at = i + lax.div(i, 12) * (lax.rem(i + 2, 4) - lax.rem(i, 4))
+        c = lax.div(at, 4)
+        side = lax.rem(lax.div(at, 2), 2)
+        zz = zpos - (1 - side) * (c + 1) + side * lax.rem(c + 1, far)
+        who = dev(zz, lax.rem(at, 2))
+        remote(sent.at[0, pl.ds(0, cap)], back.at[who], back_s.at[0], back_r.at[at], dev(zpos, 1 - core)).wait_recv()
+        loads = [pltpu.make_async_copy(back.at[who], three.at[pl.ds(r * cap, cap)], th_sem.at[r]) for r in range(3)]
+        for copy in loads:
+            copy.start()
+        mix = jnp.zeros((cap, tokens), F32)
+        for k in range(top_k):
+            mix = jnp.where(slot_row == slot_out[who, k:k + 1, :], gates[k:k + 1, :], mix)
+        high = mix.astype(BF16)
+        rest = mix - high.astype(F32)
+        mid = rest.astype(BF16)
+        low = (rest - mid.astype(F32)).astype(BF16)
+        parts = jnp.concatenate([high, mid, low], axis=0)
+        for copy in loads:
+            copy.wait()
+
+        def add(t, inner):
+            cols = pl.ds(pl.multiple_of(t * 512, 512), 512)
+            acc[:, cols] += lax.dot_general(parts, three[:, cols], (((0,), (0,)), ((), ())), preferred_element_type=F32)
+            return inner
+
+        lax.fori_loop(0, width // 512, add, 0)
+        return carry
+
+    lax.fori_loop(0, group, combine, 0)
+    row = lax.broadcasted_iota(jnp.int32, (tokens, width), 0)
+    y_ref[...] = jnp.where(row < len_ref[0], acc[...], 0.0).astype(BF16)
+
+    for i in range(1, group):
+        tk_copy(i, me).wait_send()
+    for way in range(2):
+        for hop in range(1, far + 1):
+            for part in range(2):
+                if in_ring(way, hop, part):
+                    ring_copy(way, hop, part, True).wait_send()
+                    sib_copy(way, hop, part, core).wait_send()
+    own_copy(core).wait_send()
+    for c in range(3):
+        for j in range(4):
+            send_back(jnp.int32(c), jnp.int32(j), source(jnp.int32(c), jnp.int32(j))).wait_send()
+    for j in range(2):
+        send_back(jnp.int32(3), jnp.int32(j), source(jnp.int32(3), jnp.int32(j))).wait_send()
+    send_back(jnp.int32(3), 3 - core, dev(zpos, 1 - core)).wait_send()
+
+
+EVENTS = ((0, 16, 2, 0), (0, 40, 2, 1), (1, 4, 3, 0), (1, 24, 3, 1), (1, 43, 4, 0), (1, 43, 4, 1))
+
+
+def moe_layer(group, u, h, topk, chunk_len, w_router, wsg, wsu, wsd, wg, wu, wd):
+    tokens, width = u.shape
+    top_k = topk.shape[1]
+    local, _, ff = wg.shape
+    shared_ff = wsg.shape[1]
+    experts = w_router.shape[1]
+    cap = tokens * top_k // group
+    length = jnp.broadcast_to(chunk_len.reshape(1, 1), (SUB - top_k, tokens))
+    tk = jnp.concatenate([topk.T, length], axis=0)
+    dims = (group, tokens, width, cap, local, ff, shared_ff, top_k, experts)
+    far = group // 4
+    vmem = pl.BlockSpec(memory_space=pltpu.VMEM)
+    hbm = pl.BlockSpec(memory_space=pl.ANY)
+    smem = pl.BlockSpec(memory_space=pltpu.SMEM)
+    dma = pltpu.SemaphoreType.DMA
+    scratch = [
+        pltpu.VMEM((group, SUB, tokens), jnp.int32),
+        pltpu.VMEM((group, SUB, tokens), F32),
+        pltpu.VMEM((group, SUB, tokens), F32),
+        pltpu.VMEM((SUB, tokens), F32),
+        pltpu.VMEM((tokens, shared_ff), BF16),
+        pltpu.VMEM((4 * cap, width), BF16),
+        pltpu.VMEM((4 * cap, local * ff), BF16),
+        pltpu.VMEM((4, 4 * cap, width), BF16),
+        pltpu.VMEM((4 * cap, LANES), F32),
+        pltpu.VMEM((tokens, width), F32),
+        pltpu.VMEM((4, width, 2 * LANES), BF16),
+        pltpu.VMEM((3, local * ff, 256), BF16),
+        pltpu.VMEM((2, tokens, width), BF16),
+        pltpu.VMEM((3 * cap, width), BF16),
+        dma((group,)), dma((group,)),
+        dma((2, far, 2)), dma((2, far, 2)),
+        dma((2, far, 2)), dma((2, far, 2)),
+        dma, dma,
+        dma((group,)), dma((group,)),
+        dma((4, 2)), dma((3,)), dma((2,)), dma((3,)), dma((1,)),
+    ]
+    return pl.pallas_call(
+        functools.partial(moe_kernel, dims),
+        out_shape=[jax.ShapeDtypeStruct((tokens, width), BF16), jax.ShapeDtypeStruct((group, tokens, width), BF16), jax.ShapeDtypeStruct((group, cap, width), BF16)],
+        in_specs=[vmem, vmem, vmem, smem, vmem] + [hbm] * 6,
+        out_specs=[vmem, hbm, hbm],
+        scratch_shapes=scratch,
+        compiler_params=pltpu.CompilerParams(collective_id=0, has_side_effects=True, vmem_limit_bytes=67043328),
+    )(u, h, tk, chunk_len.reshape(1), w_router.T, wsg, wsu, wsd, wg, wu, wd.reshape(local * ff, width))[0]
 
 
 def solution(mesh):
@@ -94,38 +477,10 @@
 
     def device_step(x_in, chunk_len, ctx_len, lat_cache, rope_cache, topk_idx, g_attn, w_q, w_dkv, g_kv, w_kr, w_uk, w_uv, w_o, g_ffn, w_router, w_sh_gate, w_sh_up, w_sh_down, w_exp_gate, w_exp_up, w_exp_down):
         hidden, lat_upd, rope_upd = attention_block(x_in, chunk_len, ctx_len, lat_cache, rope_cache, g_attn, w_q, w_dkv, g_kv, w_kr, w_uk, w_uv, w_o)
-        chunk = hidden.shape[2]
-        width = hidden.shape[3]
-        tokens = hidden.shape[1] * chunk
-        top_k = topk_idx.shape[-1]
-        local_exp = w_exp_gate.shape[0]
-        capacity = tokens * top_k // group
-        flat_h = hidden.reshape(tokens, width)
-        normed, route_prob, shared_out = router_and_shared(flat_h, g_ffn, w_router, w_sh_gate, w_sh_up, w_sh_down)
-        valid = (jnp.arange(chunk)[None, :] < chunk_len[0][:, None]).reshape(tokens)
-        choice = topk_idx.reshape(tokens, top_k)
-        gates = jnp.take_along_axis(route_prob, choice, axis=1)
-        flat_choice = choice.reshape(tokens * top_k)
-        target = flat_choice // local_exp
-        hits = (target[:, None] == jnp.arange(group)[None, :]).astype(jnp.int32)
-        rank_in = jnp.sum(jnp.cumsum(hits, axis=0) * hits, axis=1) - 1
-        slot = target * capacity + rank_in
-        pair_of_slot = jnp.argsort(slot)
-        pair_valid = jnp.repeat(valid, top_k)
-        expert_key = jnp.where(pair_valid, flat_choice % local_exp, local_exp).astype(jnp.int32)
-        send_rows = normed[pair_of_slot // top_k]
-        send_key = expert_key[pair_of_slot]
-        recv_rows = lax.all_to_all(send_rows, 'dpa', 0, 0, tiled=True)
-        recv_key = lax.all_to_all(send_key, 'dpa', 0, 0, tiled=True)
-        order = jnp.argsort(recv_key, stable=True)
-        sizes = jnp.bincount(recv_key, length=local_exp + 1)[:local_exp].astype(jnp.int32)
-        sorted_out = expert_ffn(recv_rows[order], sizes, w_exp_gate, w_exp_up, w_exp_down)
-        expert_rows = sorted_out[jnp.argsort(order)]
-        back_rows = lax.all_to_all(expert_rows, 'dpa', 0, 0, tiled=True)
-        pair_out = back_rows[slot].reshape(tokens, top_k, width)
-        routed = jnp.sum(gates[:, :, None] * pair_out.astype(jnp.float32), axis=1)
-        total = flat_h.astype(jnp.float32) + shared_out + routed
-        result = jnp.where(valid[:, None], total, 0.0).astype(jnp.bfloat16)
+        chunk, width = hidden.shape[2:]
+        flat_h = hidden.reshape(chunk, width)
+        normed = rms_norm(flat_h, g_ffn)
+        result = moe_layer(group, normed, flat_h, topk_idx.reshape(chunk, topk_idx.shape[-1]), chunk_len, w_router, w_sh_gate, w_sh_up, w_sh_down, w_exp_gate, w_exp_up, w_exp_down)
         return result.reshape(hidden.shape), lat_upd, rope_upd
 
     return jax.shard_map(device_step, mesh=mesh, in_specs=(tok_spec,) * 6 + (whole,) * 13 + (exp_spec,) * 3, out_specs=(tok_spec, tok_spec, tok_spec), check_vma=False)

time: 859 us -> 519 us (0.60)
  the two profiles are of different devices: /device:TPU:21 before, /device:TPU:151 now
where the time goes in v1:
time: 519 us; the launch traced here: 517 us
  Pallas kernels  395 us (76%)
  matrix products  93.2 us (18%)
  other arithmetic  14.2 us (3%)
  local copies, waits for them, and re-layouts  12.5 us (2%)
    pallas_call x1, Pallas kernels, moe_layer(): pl.pallas_call(functools.partial(moe_kernel, dims), out_shape=[jax.ShapeD...  395 us
    dot_general x1, matrix products, attention_block(): jnp.einsum('rbchk,khv->brchv', out_lat, w_uv, preferred_element_type=jnp....  25 us
    sub x1, matrix products, one_request(): attn_prob = jax.nn.softmax(scores, axis=-1).astype(jnp.bfloat16)  18.3 us
    dot_general x1, matrix products, one_request(): jnp.einsum('bchp,blp->bchl', q_rope_req, rope_req, preferred_element_type...  15.6 us
    dot_general x1, matrix products, one_request(): jnp.einsum('bchk,blk->bchl', q_lat_req, lat_req, preferred_element_type=j...  14.3 us

profile of v1, /device:TPU:151, one launch (start us, length us, event | category | flops | bytes accessed | tf_op | source)
XLA Modules:
  0.0 517.2 jit_solution(17962444404163365950)
XLA Ops:
  0.7 1.0 copy.47
  1.7 1.2 copy.46
  4.3 0.7 add_clamp_fusion
  6.3 2.6 and_reduce_fusion
  8.9 0.7 convert_element_type.115
  10.6 0.7 convolution_bitcast_fusion
  11.6 0.9 multiply_cosine_fusion.1
  12.5 2.0 fusion.52
  14.5 1.3 scatter.9
  15.7 1.0 iota_compare_fusion
  16.8 2.7 multiply_reduce_fusion
  19.5 2.2 fusion.36
  21.7 3.0 scatter.6
  24.8 9.9 %fusion.64 = f32[384,3072]{0,1:S(1)} fusion(bf16[2048,3072]{0,1:T(8,128)(2,1)} %bitcast.114, bf16[1,1,384,2048]{3,2,1,0:T(8,128)(2,1)S(1)} %copy-done.5, f32[2048]{0:T(1024)S(1)} %convert_element_type.107, f32[384]{0:T(512)S(1)} %add_rsqrt_fusion.2), kind=kOutput, calls=%fused_computation.83 | convolution fusion | flops 4834983936 | bytes 18884096
  35.5 1.2 fusion.37
  36.6 14.3 %fusion.2 = f32[384,16,1024]{2,0,1:T(8,128)} fusion(bf16[512,16,128]{2,1,0:T(8,128)(2,1)} %param.37, bf16[1,1,384,16,192]{2,4,3,1,0:T(8,128)(2,1)S(1)} %convert_bitcast_fusion, bf16[1,1,1024,512]{3,2,1,0:T(8,128)(2,1)S(1)} %scatter.6), kind=kOutput, calls=%fused_computation.5 | convolution fusion | flops 7250903040 | bytes 29884416 | tf_op jit(solution)/shard_map/while/body/eval_jaxpr/bchk,blk->bchl/dot_general | solution.py:65
  51.0 18.3 %fusion.67 = f32[384,16]{0,1:T(8,128)S(1)} fusion(f32[384,16,1024]{2,0,1:T(8,128)} %fusion.2, pred[384,1024]{1,0:T(8,128)(4,1)} %iota_compare_fusion, bf16[384,16,32]{0,2,1:T(8,128)(2,1)} %get-tuple-element.76, bf16[384,16,32]{0,2,1:T(8,128)(2,1)} %get-tuple-element.75, bf16[1,1,1024,64]{2,3,1,0:T(8,128)(2,1)S(1)} %scatter.9), kind=kOutput, calls=%fused_computation.85 | convolution fusion | flops 838337536 | bytes 26501120 | tf_op jit(solution)/shard_map/while/body/eval_jaxpr/sub | solution.py:68
  69.4 15.6 %multiply_select_fusion = f32[384,16,1024]{2,0,1:T(8,128)} fusion(f32[384,16,1024]{2,0,1:T(8,128)} %fusion.2, pred[384,1024]{1,0:T(8,128)(4,1)S(1)} %copy-done.4, bf16[384,16,32]{0,2,1:T(8,128)(2,1)S(1)} %copy-done.3, bf16[384,16,32]{0,2,1:T(8,128)(2,1)S(1)} %copy-done.2, bf16[1,1,1024,64]{2,3,1,0:T(8,128)(2,1)S(1)} %scatter.9), kind=kOutput, calls=%fused_computation.3 | convolution fusion | flops 825753600 | bytes 51642368 | tf_op jit(solution)/shard_map/while/body/eval_jaxpr/bchp,blp->bchl/dot_general | solution.py:65
  84.9 25.0 %fusion.21 = bf16[16,384,128]{2,1,0:T(8,128)(2,1)} fusion(bf16[512,16,128]{2,1,0:T(8,128)(2,1)} %param.38, f32[384,16]{0,1:T(8,128)S(1)} %fusion.67, bf16[1,1,1024,512]{3,2,1,0:T(8,128)(2,1)S(1)} %scatter.6, f32[384,16,1024]{2,0,1:T(8,128)} %multiply_select_fusion), kind=kOutput, calls=%fused_computation.29 | convolution fusion | flops 7270571008 | bytes 29908992 | tf_op jit(solution)/shard_map/rbchk,khv->brchv/dot_general | solution.py:72
  109.9 6.7 %fusion.9 = (f32[384]{0:T(512)S(1)}, bf16[384,2048]{1,0:T(8,128)(2,1)S(1)}) fusion(bf16[16,128,2048]{2,1,0:T(8,128)(2,1)} %param.39, bf16[16,384,128]{2,1,0:T(8,128)(2,1)} %fusion.21, bf16[1,1,384,2048]{3,2,1,0:T(8,128)(2,1)S(1)} %copy-done.6), kind=kOutput, calls=%fused_computation.16 | convolution fusion | flops 3227516416 | bytes 13108736 | tf_op jit(solution)/shard_map/brchv,hvd->brcd/dot_general | solution.py:73
  116.7 1.1 copy-done
  117.8 1.6 fusion.11.u_ref
  119.4 395.1 %shard_map.229 = (bf16[384,2048]{1,0:T(8,128)(2,1)}, bf16[16,384,2048]{2,1,0:T(8,128)(2,1)}, bf16[16,144,2048]{2,1,0:T(8,128)(2,1)}) custom-call(bf16[384,2048]{1,0:T(8,128)(2,1)} %fusion.11.u_ref, bf16[384,2048]{1,0:T(8,128)(2,1)} %copy-done, s32[8,384]{1,0:T(8,128)} %concatenate.57.tk_ref, s32[1]{0:T(128)} %bitcast.107.len_ref, ...), custom_call_target="tpu_custom_call" | custom-call | tf_op jit(solution)/shard_map/pallas_call | solution.py:462
  514.5 2.7 copy.48
  (44 shorter events, 3.4 us)
Async XLA Ops:
  0.6 8.9 %copy-start.5 = (bf16[1,1,384,2048]{3,2,1,0:T(8,128)(2,1)S(1)}, bf16[1,1,384,2048]{3,2,1,0:T(8,128)(2,1)}, u32[]{:S(2)}) copy-start(bf16[1,1,384,2048]{3,2,1,0:T(8,128)(2,1)} %param.26) | copy-start | bytes 4718596
  0.6 9.4 %copy-start.10 = (s32[1,1,384,6]{2,1,3,0:T(1,128)S(1)}, s32[1,1,384,6]{2,1,3,0:T(1,128)}, u32[]{:S(2)}) copy-start(s32[1,1,384,6]{2,1,3,0:T(1,128)} %param.31) | copy-start | bytes 27652
  0.7 9.3 %copy-start.11 = (bf16[2048]{0:T(1024)(128)(2,1)S(1)}, bf16[2048]{0:T(1024)(128)(2,1)}, u32[]{:S(2)}) copy-start(bf16[2048]{0:T(1024)(128)(2,1)} %param.32) | copy-start | bytes 12292
  0.7 10.0 %copy-start.13 = (bf16[2048,64]{0,1:T(8,128)(2,1)S(1)}, bf16[2048,64]{0,1:T(8,128)(2,1)}, u32[]{:S(2)}) copy-start(bf16[2048,64]{0,1:T(8,128)(2,1)} %param.36) | copy-start | bytes 786436
  0.7 9.3 %copy-start.12 = (bf16[2048]{0:T(1024)(128)(2,1)S(1)}, bf16[2048]{0:T(1024)(128)(2,1)}, u32[]{:S(2)}) copy-start(bf16[2048]{0:T(1024)(128)(2,1)} %param.40) | copy-start | bytes 12292
  15.7 53.6 %copy-start.7 = (bf16[1,1,1024,64]{2,3,1,0:T(8,128)(2,1)}, bf16[1,1,1024,64]{2,3,1,0:T(8,128)(2,1)S(1)}, u32[]{:S(2)}) copy-start(bf16[1,1,1024,64]{2,3,1,0:T(8,128)(2,1)S(1)} %scatter.9) | copy-start | bytes 393220
  24.7 60.2 %copy-start.1 = (bf16[1,1,1024,512]{3,2,1,0:T(8,128)(2,1)}, bf16[1,1,1024,512]{3,2,1,0:T(8,128)(2,1)S(1)}, u32[]{:S(2)}) copy-start(bf16[1,1,1024,512]{3,2,1,0:T(8,128)(2,1)S(1)} %scatter.6) | copy-start | bytes 3145732
  34.7 0.8 copy-start.8
  34.7 0.8 copy-start.9
  51.0 18.4 %copy-start.2 = (bf16[384,16,32]{0,2,1:T(8,128)(2,1)S(1)}, bf16[384,16,32]{0,2,1:T(8,128)(2,1)}, u32[]{:S(2)}) copy-start(bf16[384,16,32]{0,2,1:T(8,128)(2,1)} %get-tuple-element.75) | copy-start | bytes 1179652
  51.0 18.4 %copy-start.3 = (bf16[384,16,32]{0,2,1:T(8,128)(2,1)S(1)}, bf16[384,16,32]{0,2,1:T(8,128)(2,1)}, u32[]{:S(2)}) copy-start(bf16[384,16,32]{0,2,1:T(8,128)(2,1)} %get-tuple-element.76) | copy-start | bytes 1179652
  51.0 18.4 %copy-start.4 = (pred[384,1024]{1,0:T(8,128)(4,1)S(1)}, pred[384,1024]{1,0:T(8,128)(4,1)}, u32[]{:S(2)}) copy-start(pred[384,1024]{1,0:T(8,128)(4,1)} %iota_compare_fusion) | copy-start | bytes 1179652
  84.9 25.0 %copy-start.6 = (bf16[1,1,384,2048]{3,2,1,0:T(8,128)(2,1)S(1)}, bf16[1,1,384,2048]{3,2,1,0:T(8,128)(2,1)}, u32[]{:S(2)}) copy-start(bf16[1,1,384,2048]{3,2,1,0:T(8,128)(2,1)} %param.26) | copy-start | bytes 4718596
  116.6 1.1 copy-start

commit v2 on v1

--- a/solution.py
+++ b/solution.py
@@ -9,72 +9,6 @@
 
 EPS = 1e-6
 THETA = 10000.0
-
-
-def rms_norm(vals, gain):
-    vals_f32 = vals.astype(jnp.float32)
-    inv_rms = lax.rsqrt(jnp.mean(vals_f32 * vals_f32, axis=-1, keepdims=True) + EPS)
-    return (vals_f32 * inv_rms * gain.astype(jnp.float32)).astype(jnp.bfloat16)
-
-
-def rope_tables(positions, half):
-    inv_freq = THETA ** (-2.0 * jnp.arange(half, dtype=jnp.float32) / (2 * half))
-    angle = positions.astype(jnp.float32)[..., None] * inv_freq
-    return jnp.cos(angle), jnp.sin(angle)
-
-
-def rotate(vals, cos_tab, sin_tab):
-    half = cos_tab.shape[-1]
-    first = vals[..., :half]
-    second = vals[..., half:]
-    return jnp.concatenate([first * cos_tab - second * sin_tab, second * cos_tab + first * sin_tab], axis=-1)
-
-
-def write_window(cache_row, new_rows, start, keep):
-    old_rows = lax.dynamic_slice_in_dim(cache_row, start, new_rows.shape[0], axis=0)
-    merged = jnp.where(keep[:, None], new_rows, old_rows)
-    return lax.dynamic_update_slice_in_dim(cache_row, merged, start, axis=0)
-
-
-def attention_block(x_in, chunk_len, ctx_len, lat_cache, rope_cache, g_attn, w_q, w_dkv, g_kv, w_kr, w_uk, w_uv, w_o):
-    chunk = x_in.shape[2]
-    ctx_max = lat_cache.shape[2]
-    rope_dim = w_kr.shape[1]
-    nope_dim = w_q.shape[2] - rope_dim
-    scale = w_q.shape[2] ** -0.5
-    normed = rms_norm(x_in, g_attn)
-    q_full = jnp.einsum('brcd,dhq->brchq', normed, w_q, preferred_element_type=jnp.float32).astype(jnp.bfloat16)
-    positions = ctx_len[:, :, None] + jnp.arange(chunk)
-    cos_tab, sin_tab = rope_tables(positions, rope_dim // 2)
-    q_rope = rotate(q_full[..., nope_dim:].astype(jnp.float32), cos_tab[..., None, :], sin_tab[..., None, :]).astype(jnp.bfloat16)
-    q_lat = jnp.einsum('brchn,khn->brchk', q_full[..., :nope_dim], w_uk, preferred_element_type=jnp.float32).astype(jnp.bfloat16)
-    lat_new = rms_norm(jnp.einsum('brcd,dk->brck', normed, w_dkv, preferred_element_type=jnp.float32), g_kv)
-    rope_new = rotate(jnp.einsum('brcd,dp->brcp', normed, w_kr, preferred_element_type=jnp.float32), cos_tab, sin_tab).astype(jnp.bfloat16)
-    keep = jnp.arange(chunk) < chunk_len[:, :, None]
-    writer = jax.vmap(jax.vmap(write_window))
-    lat_upd = writer(lat_cache, lat_new, ctx_len, keep)
-    rope_upd = writer(rope_cache, rope_new, ctx_len, keep)
-    key_pos = jnp.arange(ctx_max)
-
-    def one_request(index):
-        q_lat_req = lax.dynamic_index_in_dim(q_lat, index, axis=1, keepdims=False)
-        q_rope_req = lax.dynamic_index_in_dim(q_rope, index, axis=1, keepdims=False)
-        lat_req = lax.dynamic_index_in_dim(lat_upd, index, axis=1, keepdims=False)
-        rope_req = lax.dynamic_index_in_dim(rope_upd, index, axis=1, keepdims=False)
-        pos_req = lax.dynamic_index_in_dim(positions, index, axis=1, keepdims=False)
-        scores = (jnp.einsum('bchk,blk->bchl', q_lat_req, lat_req, preferred_element_type=jnp.float32) + jnp.einsum('bchp,blp->bchl', q_rope_req, rope_req, preferred_element_type=jnp.float32)) * scale
-        visible = key_pos[None, None, None, :] <= pos_req[:, :, None, None]
-        scores = jnp.where(visible, scores, -1e30)
-        attn_prob = jax.nn.softmax(scores, axis=-1).astype(jnp.bfloat16)
-        return jnp.einsum('bchl,blk->bchk', attn_prob, lat_req, preferred_element_type=jnp.float32).astype(jnp.bfloat16)
-
-    out_lat = lax.map(one_request, jnp.arange(x_in.shape[1]))
-    out_head = jnp.einsum('rbchk,khv->brchv', out_lat, w_uv, preferred_element_type=jnp.float32).astype(jnp.bfloat16)
-    attn_out = jnp.einsum('brchv,hvd->brcd', out_head, w_o, preferred_element_type=jnp.float32).astype(jnp.bfloat16)
-    hidden = (x_in.astype(jnp.float32) + attn_out.astype(jnp.float32)).astype(jnp.bfloat16)
-    return hidden, lat_upd, rope_upd
-
-
 MESH_ID = pl.DeviceIdType.MESH
 F32 = jnp.float32
 BF16 = jnp.bfloat16
@@ -82,14 +16,157 @@
 SUB = 8
 
 
-def moe_kernel(dims, u_ref, h_ref, tk_ref, len_ref, wr_ref, wsg, wsu, wsd, wg, wu, wd, y_ref, rows_all, back, tk_all, slot_in, slot_out, gates, sh_act, picked, act, sent, row_exp, acc, w_gu, w_dn, stage, three, tk_s, tk_r, ring_s, ring_r, sib_s, sib_r, own_s, own_r, back_s, back_r, gu_sem, dn_sem, st_sem, th_sem, loc_sem):
+def rms_norm(vals, gain):
+    vals_f32 = vals.astype(jnp.float32)
+    inv_rms = lax.rsqrt(jnp.mean(vals_f32 * vals_f32, axis=-1, keepdims=True) + EPS)
+    return (vals_f32 * inv_rms * gain.astype(jnp.float32)).astype(jnp.bfloat16)
+
+
+def rope_tables(positions, half):
+    inv_freq = THETA ** (-2.0 * jnp.arange(half, dtype=jnp.float32) / (2 * half))
+    angle = positions.astype(jnp.float32)[..., None] * inv_freq
+    return jnp.cos(angle), jnp.sin(angle)
+
+
+def attn_kernel(scale, len_ref, ctx_ref, x_hbm, gains_ref, tab_ref, dkv_hbm, kr_hbm, q_hbm, lat_hbm, rope_hbm, uk_hbm, uv_hbm, wo_hbm, h_ref, u_ref, lat_ref, rope_ref, x, dkv, kr, q, lat_old, rope_old, uk, uv, wo, uk_wide, uv_wide, turned, lat_t, rope_rows, heads_out, sems, q_sems):
+    heads, qdim, width = q.shape
+    ctx_max, rank = lat_old.shape
+    rope_dim = rope_old.shape[0]
+    nope = qdim - rope_dim
+    half = rope_dim // 2
+    chunk = x.shape[0]
+    copies = [pltpu.make_async_copy(src, dst, sems.at[i]) for i, (src, dst) in enumerate(((x_hbm, x), (dkv_hbm, dkv), (kr_hbm, kr), (lat_hbm, lat_old), (rope_hbm, rope_old), (uk_hbm, uk), (uv_hbm, uv), (wo_hbm, wo)))]
+
+    def q_copy(i):
+        both = pl.ds(2 * i, 2)
+        return pltpu.make_async_copy(q_hbm.at[both], q.at[both], q_sems.at[i])
+
+    for copy in copies[:5]:
+        copy.start()
+    for i in range(2):
+        q_copy(i).start()
+    for copy in copies[5:7]:
+        copy.start()
+    for i in range(2, heads // 2):
+        q_copy(i).start()
+    copies[7].start()
+    clen = len_ref[0]
+    ctx = ctx_ref[0]
+    cos_tab = tab_ref[:half, :]
+    sin_tab = tab_ref[half:, :]
+
+    def roped(vals):
+        first = vals[:half]
+        second = vals[half:]
+        return jnp.concatenate([first * cos_tab - second * sin_tab, second * cos_tab + first * sin_tab], axis=0).astype(BF16)
+
+    def normed(vals, gain):
+        return vals * lax.rsqrt(jnp.mean(vals * vals, axis=1, keepdims=True) + EPS) * gain
+
+    copies[0].wait()
+    a = normed(x[...].astype(F32), gains_ref[:, :width]).astype(BF16)
+    turned[...] = jnp.transpose(a.astype(F32)).astype(BF16)
+    copies[1].wait()
+    lat_new = normed(jnp.dot(a, dkv[...], preferred_element_type=F32), gains_ref[:, 2 * width:]).astype(BF16)
+    copies[2].wait()
+    rope_new = roped(jnp.dot(kr[...], turned[...], preferred_element_type=F32))
+    place = lax.broadcasted_iota(jnp.int32, (ctx_max, chunk), 0) - ctx
+    row = lax.broadcasted_iota(jnp.int32, (ctx_max, chunk), 1)
+    move = jnp.where(jnp.logical_and(place == row, row < clen), 1.0, 0.0).astype(BF16)
+    pos = lax.broadcasted_iota(jnp.int32, (ctx_max, rank), 0) - ctx
+    copies[3].wait()
+    lat = jnp.where(jnp.logical_and(pos >= 0, pos < clen), jnp.dot(move, lat_new, preferred_element_type=F32), lat_old[...].astype(F32))
+    lat_ref[...] = lat.astype(BF16)
+    lat_t[...] = jnp.transpose(lat).astype(BF16)
+    place = lax.broadcasted_iota(jnp.int32, (chunk, ctx_max), 1) - ctx
+    row = lax.broadcasted_iota(jnp.int32, (chunk, ctx_max), 0)
+    move = jnp.where(jnp.logical_and(place == row, row < clen), 1.0, 0.0).astype(BF16)
+    pos = lax.broadcasted_iota(jnp.int32, (rope_dim, ctx_max), 1) - ctx
+    copies[4].wait()
+    rope = jnp.where(jnp.logical_and(pos >= 0, pos < clen), jnp.dot(rope_new, move, preferred_element_type=F32), rope_old[...].astype(F32))
+    rope_ref[...] = rope.astype(BF16)
+    rope_rows[...] = jnp.transpose(jnp.concatenate([rope, jnp.zeros_like(rope)], axis=0)).astype(BF16)
+    copies[5].wait()
+    uk_wide[...] = uk[...].astype(F32)
+    copies[6].wait()
+    uv_wide[...] = uv[...].astype(F32)
+    seen = lax.broadcasted_iota(jnp.int32, (ctx_max, chunk), 0) - lax.broadcasted_iota(jnp.int32, (ctx_max, chunk), 1) <= ctx
+    factor = scale * 1.4426950408889634
+
+    def pair(i, carry):
+        q_copy(i).wait()
+        both = jnp.dot(q[pl.ds(2 * i, 2)].reshape(2 * qdim, width), turned[...], preferred_element_type=F32).astype(BF16)
+        lats = []
+        ropes = []
+        for k in range(2):
+            mine = both[k * qdim:(k + 1) * qdim]
+            up = uk_wide[pl.ds(2 * i + k, rank, stride=heads), :].astype(BF16)
+            lats.append(jnp.dot(up, mine[:nope], preferred_element_type=F32).astype(BF16))
+            ropes.append(roped(mine[nope:].astype(F32)))
+        ropes = jnp.concatenate(ropes, axis=1)
+        scores = jnp.dot(lat_ref[...], jnp.concatenate(lats, axis=1), preferred_element_type=F32) + jnp.dot(rope_rows[:, :rope_dim], ropes, preferred_element_type=F32)
+        probs = []
+        for k in range(2):
+            mine = jnp.where(seen, scores[:, k * chunk:(k + 1) * chunk], -1e30)
+            weight = jnp.exp2((mine - jnp.max(mine, axis=0, keepdims=True)) * factor)
+            probs.append((weight * (1.0 / jnp.sum(weight, axis=0, keepdims=True))).astype(BF16))
+        out = jnp.dot(lat_t[...], jnp.concatenate(probs, axis=1), preferred_element_type=F32).astype(BF16)
+        for k in range(2):
+            up = uv_wide[pl.ds(2 * i + k, rank, stride=heads), :].astype(BF16)
+            mine = lax.dot_general(out[:, k * chunk:(k + 1) * chunk], up, (((0,), (0,)), ((), ())), preferred_element_type=F32)
+            heads_out[:, pl.ds(pl.multiple_of((2 * i + k) * nope, nope), nope)] = mine.astype(BF16)
+        return carry
+
+    lax.fori_loop(0, heads // 2, pair, 0)
+    copies[7].wait()
+
+    def project(t, total):
+        cols = pl.ds(pl.multiple_of(t * 256, 256), 256)
+        out = jnp.dot(heads_out[...], wo[:, cols], preferred_element_type=F32).astype(BF16)
+        hidden = (x[:, cols].astype(F32) + out.astype(F32)).astype(BF16)
+        h_ref[:, cols] = hidden
+        wide_h = hidden.astype(F32)
+        return total + jnp.sum(wide_h * wide_h, axis=1, keepdims=True)
+
+    total = lax.fori_loop(0, width // 256, project, jnp.zeros((chunk, 1), F32))
+    inv = lax.rsqrt(total / width + EPS)
+    u_ref[...] = (h_ref[...].astype(F32) * inv * gains_ref[:, width:2 * width]).astype(BF16)
+
+
+def attention_block(x, chunk_len, ctx_len, lat_cache, rope_cache, g_attn, w_q, w_dkv, g_kv, w_kr, w_uk, w_uv, w_o, g_ffn):
+    chunk, width = x.shape
+    ctx_max, rank = lat_cache.shape
+    rope_dim = rope_cache.shape[1]
+    heads, qdim = w_q.shape[1:]
+    nope = qdim - rope_dim
+    vdim = w_uv.shape[2]
+    tab = jnp.concatenate(rope_tables(ctx_len.reshape(1) + jnp.arange(chunk), rope_dim // 2), axis=1).T
+    gains = jnp.concatenate([g_attn, g_ffn, g_kv]).astype(F32).reshape(1, 2 * width + rank)
+    vmem = pl.BlockSpec(memory_space=pltpu.VMEM)
+    hbm = pl.BlockSpec(memory_space=pl.ANY)
+    smem = pl.BlockSpec(memory_space=pltpu.SMEM)
+    low = [(chunk, width), (width, rank), (rope_dim, width), (heads, qdim, width), (ctx_max, rank), (rope_dim, ctx_max), (rank * heads, nope), (rank * heads, vdim), (heads * vdim, width)]
+    wide = [(rank * heads, nope), (rank * heads, vdim)]
+    more = [(width, chunk), (rank, ctx_max), (ctx_max, 2 * rope_dim), (chunk, heads * vdim)]
+    hidden, normed, lat, rope = pl.pallas_call(
+        functools.partial(attn_kernel, qdim ** -0.5),
+        out_shape=[jax.ShapeDtypeStruct((chunk, width), BF16), jax.ShapeDtypeStruct((chunk, width), BF16), jax.ShapeDtypeStruct((ctx_max, rank), BF16), jax.ShapeDtypeStruct((rope_dim, ctx_max), BF16)],
+        in_specs=[smem, smem, hbm, vmem, vmem] + [hbm] * 8,
+        out_specs=[vmem] * 4,
+        scratch_shapes=[pltpu.VMEM(shape, BF16) for shape in low] + [pltpu.VMEM(shape, F32) for shape in wide] + [pltpu.VMEM(shape, BF16) for shape in more] + [pltpu.SemaphoreType.DMA((8,)), pltpu.SemaphoreType.DMA((heads // 2,))],
+        compiler_params=pltpu.CompilerParams(vmem_limit_bytes=67043328),
+    )(chunk_len.reshape(1), ctx_len.reshape(1), x, gains, tab, w_dkv, w_kr.T, w_q.transpose(1, 2, 0), lat_cache, rope_cache.T, w_uk.reshape(rank * heads, nope), w_uv.reshape(rank * heads, vdim), w_o.reshape(heads * vdim, width))
+    return hidden, normed, lat, rope.T
+
+
+def moe_kernel(dims, u_ref, h_ref, tk_ref, len_ref, wr_ref, wsg, wsu, wsd, wg, wu, wd, y_ref, rows_all, tk_all, slot_in, slot_out, gates, sh_act, picked, act, sent, row_exp, acc, w_gu, w_dn, stage, three, back, halfway, tk_s, tk_r, ring_s, ring_r, sib_s, sib_r, own_s, own_r, back_s, back_r, leg_s, leg_r, fwd_s, gu_sem, dn_sem, st_sem, loc_sem):
     group, tokens, width, cap, local, ff, shared_ff, top_k, experts = dims
     ring = group // 2
     half = tokens // 2
     chunk_rows = 4 * cap
-    gu_tiles = local * ff // LANES
+    gu_tiles = local * ff // (2 * LANES)
     per_exp = ff // LANES
-    sh_tiles = shared_ff // LANES
+    sh_tiles = shared_ff // (2 * LANES)
     dn_cols = w_dn.shape[2]
     dn_tiles = width // dn_cols
     me = lax.axis_index('dpa')
@@ -159,13 +236,17 @@
     def gu_copies(shared, t):
         slot = lax.rem(t, w_gu.shape[0])
         if shared:
-            cols = pl.ds(pl.multiple_of(t * LANES, LANES), LANES)
+            cols = pl.ds(pl.multiple_of(t * 2 * LANES, 2 * LANES), 2 * LANES)
             srcs = (wsg.at[:, cols], wsu.at[:, cols])
         else:
-            cols = pl.ds(pl.multiple_of(lax.rem(t, per_exp) * LANES, LANES), LANES)
-            exp = lax.div(t, per_exp)
-            srcs = (wg.at[exp, :, cols], wu.at[exp, :, cols])
-        return [pltpu.make_async_copy(src, w_gu.at[slot, :, pl.ds(i * LANES, LANES)], gu_sem.at[slot, i]) for i, src in enumerate(srcs)]
+            srcs = []
+            for ref in (wg, wu):
+                for part in range(2):
+                    tile = 2 * t + part
+                    cols = pl.ds(pl.multiple_of(lax.rem(tile, per_exp) * LANES, LANES), LANES)
+                    srcs.append(ref.at[lax.div(tile, per_exp), :, cols])
+        span = 4 * LANES // len(srcs)
+        return [pltpu.make_async_copy(src, w_gu.at[slot, :, pl.ds(i * span, span)], gu_sem.at[slot, i]) for i, src in enumerate(srcs)]
 
     def dn_copy(shared, t):
         slot = lax.rem(t, w_dn.shape[0])
@@ -203,8 +284,8 @@
             gates[k:k + 1, :] = jnp.zeros((1, tokens), F32)
 
     def glu(both):
-        gate = both[:, :LANES]
-        return gate * jax.nn.sigmoid(gate) * both[:, LANES:]
+        gate = both[:, :2 * LANES]
+        return gate * jax.nn.sigmoid(gate) * both[:, 2 * LANES:]
 
     def sh_gu(t, carry):
         @pl.when(t + gu_ahead < sh_tiles)
@@ -214,7 +295,7 @@
         for copy in gu_copies(True, t):
             copy.wait()
         both = jnp.dot(u_ref[...], w_gu[lax.rem(t, w_gu.shape[0])], preferred_element_type=F32)
-        sh_act[:, pl.ds(pl.multiple_of(t * LANES, LANES), LANES)] = glu(both).astype(BF16)
+        sh_act[:, pl.ds(pl.multiple_of(t * 2 * LANES, 2 * LANES), 2 * LANES)] = glu(both).astype(BF16)
         return carry
 
     lax.fori_loop(0, sh_tiles, sh_gu, 0)
@@ -270,18 +351,37 @@
 
     slot_row = lax.broadcasted_iota(jnp.int32, (cap, tokens), 0).astype(F32)
 
+    hops = (1, 2, 4, 3)
+
+    def distance(c):
+        return c + 1 + lax.div(c, 2) - 2 * lax.div(c, 3)
+
     def source(c, j):
         side = lax.div(j, 2)
-        zz = zpos + (1 - side) * (c + 1) - side * lax.rem(c + 1, far)
+        zz = zpos + (1 - side) * distance(c) - side * lax.rem(distance(c), far)
         return dev(zz, lax.rem(j, 2))
 
     def send_back(c, j, to):
-        block = sent.at[c, pl.ds(pl.multiple_of(j * cap, 16), cap)]
+        block = sent.at[lax.rem(c, 2), pl.ds(pl.multiple_of(j * cap, 16), cap)]
         return remote(block, back.at[me], back_s.at[c * 4 + j], back_r.at[c * 4 + lax.div(j, 2) * 2 + core], to)
 
+    def leg_copy(way):
+        j = core if way == 0 else 1 - core
+        block = sent.at[0, pl.ds(pl.multiple_of(j * cap, 16), cap)]
+        return remote(block, halfway.at[way], leg_s.at[way], leg_r.at[way], dev(zpos + (1 - 2 * way) * (far // 2), core))
+
+    def fwd_copy(way):
+        j = core if way == 0 else 1 - core
+        sign = 1 - 2 * way
+        origin = dev(zpos - sign * (far // 2), core)
+        return remote(halfway.at[way], back.at[origin], fwd_s.at[way], back_r.at[8 + core], dev(zpos + sign * (far // 2), j))
+
+    def to_sibling():
+        return send_back(jnp.int32(2), 3 - core, dev(zpos, 1 - core))
+
     def chunk(c, carry):
-        for hop in range(1, far + 1):
-            @pl.when(c == hop - 1)
+        for which_c, hop in enumerate(hops):
+            @pl.when(c == which_c)
             def _():
                 for part in range(2):
                     for way in range(2):
@@ -316,10 +416,17 @@
 
         lax.fori_loop(0, 4, gather, 0)
 
-        @pl.when(c > 0)
+        @pl.when(jnp.logical_and(c > 0, c < 3))
         def _():
             for j in range(4):
                 send_back(c - 1, j, source(c - 1, jnp.int32(j))).start()
+
+        @pl.when(c == 3)
+        def _():
+            for way in range(2):
+                leg_copy(way).start()
+            to_sibling().start()
+            back[me] = sent[0, pl.ds(pl.multiple_of((2 + core) * cap, 16), cap), :]
 
         def gate_up(t, inner):
             @pl.when(t + gu_ahead < gu_tiles)
@@ -333,9 +440,18 @@
                 def _():
                     relay(hop, part)
 
+            @pl.when(jnp.logical_and(c == 3, t == HAND_ON * gu_tiles // 44))
+            def _():
+                for way in range(2):
+                    leg_copy(way).wait_recv()
+                    fwd_copy(way).start()
+
             both = jnp.dot(picked[...], w_gu[lax.rem(t, w_gu.shape[0])], preferred_element_type=F32)
-            mine = row_exp[...] == lax.div(t, per_exp).astype(F32)
-            act[:, pl.ds(pl.multiple_of(t * LANES, LANES), LANES)] = jnp.where(mine, glu(both), 0.0).astype(BF16)
+            mixed = glu(both)
+            for part in range(2):
+                tile = 2 * t + part
+                mine = row_exp[...] == lax.div(tile, per_exp).astype(F32)
+                act[:, pl.ds(pl.multiple_of(tile * LANES, LANES), LANES)] = jnp.where(mine, mixed[:, part * LANES:(part + 1) * LANES], 0.0).astype(BF16)
             return inner
 
         lax.fori_loop(0, gu_tiles, gate_up, 0)
@@ -343,6 +459,13 @@
         @pl.when(c < 3)
         def _():
             prime_gu(False)
+
+        for which_c in (2, 3):
+            @pl.when(c == which_c)
+            def _():
+                for j in range(4):
+                    before_last = jnp.int32(which_c - 2)
+                    send_back(before_last, jnp.int32(j), source(before_last, jnp.int32(j))).wait_send()
 
         def down(t, inner):
             @pl.when(t + dn_ahead < dn_tiles)
@@ -351,7 +474,7 @@
 
             dn_copy(False, t).wait()
             out = jnp.dot(act[...], w_dn[lax.rem(t, w_dn.shape[0])], preferred_element_type=F32)
-            sent[c, :, pl.ds(pl.multiple_of(t * dn_cols, dn_cols), dn_cols)] = out.astype(BF16)
+            sent[lax.rem(c, 2), :, pl.ds(pl.multiple_of(t * dn_cols, dn_cols), dn_cols)] = out.astype(BF16)
             return inner
 
         lax.fori_loop(0, dn_tiles, down, 0)
@@ -363,41 +486,39 @@
         return carry
 
     lax.fori_loop(0, 4, chunk, 0)
-    for j in range(2):
+    for j in range(4):
         send_back(jnp.int32(3), jnp.int32(j), source(jnp.int32(3), jnp.int32(j))).start()
-    send_back(jnp.int32(3), 3 - core, dev(zpos, 1 - core)).start()
-    mine = pltpu.make_async_copy(sent.at[3, pl.ds(pl.multiple_of((2 + core) * cap, 16), cap)], back.at[me], back_r.at[14 + core])
-    mine.start()
 
     def combine(i, carry):
-        at = i + lax.div(i, 12) * (lax.rem(i + 2, 4) - lax.rem(i, 4))
-        c = lax.div(at, 4)
-        side = lax.rem(lax.div(at, 2), 2)
-        zz = zpos - (1 - side) * (c + 1) + side * lax.rem(c + 1, far)
-        who = dev(zz, lax.rem(at, 2))
-        remote(sent.at[0, pl.ds(0, cap)], back.at[who], back_s.at[0], back_r.at[at], dev(zpos, 1 - core)).wait_recv()
-        loads = [pltpu.make_async_copy(back.at[who], three.at[pl.ds(r * cap, cap)], th_sem.at[r]) for r in range(3)]
-        for copy in loads:
-            copy.start()
+        c = lax.div(i, 4)
+        side = lax.rem(lax.div(i, 2), 2)
+        zz = zpos - (1 - side) * distance(c) + side * lax.rem(distance(c), far)
+        who = dev(zz, lax.rem(i, 2))
+
+        @pl.when(i != 10 + core)
+        def _():
+            remote(sent.at[0, pl.ds(0, cap)], back.at[who], back_s.at[0], back_r.at[i], dev(zpos, 1 - core)).wait_recv()
+
         mix = jnp.zeros((cap, tokens), F32)
         for k in range(top_k):
             mix = jnp.where(slot_row == slot_out[who, k:k + 1, :], gates[k:k + 1, :], mix)
-        high = mix.astype(BF16)
-        rest = mix - high.astype(F32)
-        mid = rest.astype(BF16)
-        low = (rest - mid.astype(F32)).astype(BF16)
-        parts = jnp.concatenate([high, mid, low], axis=0)
-        for copy in loads:
-            copy.wait()
+        high = mix.astype(BF16).astype(F32)
+        mid = (mix - high).astype(BF16).astype(F32)
+        low = mix - high - mid
+        parts = jnp.transpose(jnp.concatenate([high, mid, low, jnp.zeros((three.shape[0] - 3 * cap, tokens), F32)], axis=0)).astype(BF16)
+        block = back[who]
+        for r in range(3):
+            three[r * cap:(r + 1) * cap, :] = block
 
         def add(t, inner):
             cols = pl.ds(pl.multiple_of(t * 512, 512), 512)
-            acc[:, cols] += lax.dot_general(parts, three[:, cols], (((0,), (0,)), ((), ())), preferred_element_type=F32)
+            acc[:, cols] += jnp.dot(parts, three[:, cols], preferred_element_type=F32)
             return inner
 
         lax.fori_loop(0, width // 512, add, 0)
         return carry
 
+    three[3 * cap:, :] = jnp.zeros((three.shape[0] - 3 * cap, width), BF16)
     lax.fori_loop(0, group, combine, 0)
     row = lax.broadcasted_iota(jnp.int32, (tokens, width), 0)
     y_ref[...] = jnp.where(row < len_ref[0], acc[...], 0.0).astype(BF16)
@@ -411,15 +532,16 @@
                     ring_copy(way, hop, part, True).wait_send()
                     sib_copy(way, hop, part, core).wait_send()
     own_copy(core).wait_send()
-    for c in range(3):
-        for j in range(4):
-            send_back(jnp.int32(c), jnp.int32(j), source(jnp.int32(c), jnp.int32(j))).wait_send()
-    for j in range(2):
+    for j in range(4):
         send_back(jnp.int32(3), jnp.int32(j), source(jnp.int32(3), jnp.int32(j))).wait_send()
-    send_back(jnp.int32(3), 3 - core, dev(zpos, 1 - core)).wait_send()
+    for way in range(2):
+        leg_copy(way).wait_send()
+        fwd_copy(way).wait_send()
+    to_sibling().wait_send()
 
 
 EVENTS = ((0, 16, 2, 0), (0, 40, 2, 1), (1, 4, 3, 0), (1, 24, 3, 1), (1, 43, 4, 0), (1, 43, 4, 1))
+HAND_ON = 34
 
 
 def moe_layer(group, u, h, topk, chunk_len, w_router, wsg, wsu, wsd, wg, wu, wd):
@@ -445,25 +567,28 @@
         pltpu.VMEM((tokens, shared_ff), BF16),
         pltpu.VMEM((4 * cap, width), BF16),
         pltpu.VMEM((4 * cap, local * ff), BF16),
-        pltpu.VMEM((4, 4 * cap, width), BF16),
+        pltpu.VMEM((2, 4 * cap, width), BF16),
         pltpu.VMEM((4 * cap, LANES), F32),
         pltpu.VMEM((tokens, width), F32),
-        pltpu.VMEM((4, width, 2 * LANES), BF16),
+        pltpu.VMEM((3, width, 4 * LANES), BF16),
         pltpu.VMEM((3, local * ff, 256), BF16),
         pltpu.VMEM((2, tokens, width), BF16),
-        pltpu.VMEM((3 * cap, width), BF16),
+        pltpu.VMEM((pl.cdiv(3 * cap, 256) * 256, width), BF16),
+        pltpu.VMEM((group, cap, width), BF16),
+        pltpu.VMEM((2, cap, width), BF16),
         dma((group,)), dma((group,)),
         dma((2, far, 2)), dma((2, far, 2)),
         dma((2, far, 2)), dma((2, far, 2)),
         dma, dma,
         dma((group,)), dma((group,)),
-        dma((4, 2)), dma((3,)), dma((2,)), dma((3,)), dma((1,)),
+        dma((2,)), dma((2,)), dma((2,)),
+        dma((3, 4)), dma((3,)), dma((2,)), dma((1,)),
     ]
     return pl.pallas_call(
         functools.partial(moe_kernel, dims),
-        out_shape=[jax.ShapeDtypeStruct((tokens, width), BF16), jax.ShapeDtypeStruct((group, tokens, width), BF16), jax.ShapeDtypeStruct((group, cap, width), BF16)],
+        out_shape=[jax.ShapeDtypeStruct((tokens, width), BF16), jax.ShapeDtypeStruct((group, tokens, width), BF16)],
         in_specs=[vmem, vmem, vmem, smem, vmem] + [hbm] * 6,
-        out_specs=[vmem, hbm, hbm],
+        out_specs=[vmem, hbm],
         scratch_shapes=scratch,
         compiler_params=pltpu.CompilerParams(collective_id=0, has_side_effects=True, vmem_limit_bytes=67043328),
     )(u, h, tk, chunk_len.reshape(1), w_router.T, wsg, wsu, wsd, wg, wu, wd.reshape(local * ff, width))[0]
@@ -476,11 +601,8 @@
     exp_spec = P('dpa')
 
     def device_step(x_in, chunk_len, ctx_len, lat_cache, rope_cache, topk_idx, g_attn, w_q, w_dkv, g_kv, w_kr, w_uk, w_uv, w_o, g_ffn, w_router, w_sh_gate, w_sh_up, w_sh_down, w_exp_gate, w_exp_up, w_exp_down):
-        hidden, lat_upd, rope_upd = attention_block(x_in, chunk_len, ctx_len, lat_cache, rope_cache, g_attn, w_q, w_dkv, g_kv, w_kr, w_uk, w_uv, w_o)
-        chunk, width = hidden.shape[2:]
-        flat_h = hidden.reshape(chunk, width)
-        normed = rms_norm(flat_h, g_ffn)
-        result = moe_layer(group, normed, flat_h, topk_idx.reshape(chunk, topk_idx.shape[-1]), chunk_len, w_router, w_sh_gate, w_sh_up, w_sh_down, w_exp_gate, w_exp_up, w_exp_down)
-        return result.reshape(hidden.shape), lat_upd, rope_upd
+        hidden, normed, lat_upd, rope_upd = attention_block(x_in[0, 0], chunk_len, ctx_len, lat_cache[0, 0], rope_cache[0, 0], g_attn, w_q, w_dkv, g_kv, w_kr, w_uk, w_uv, w_o, g_ffn)
+        result = moe_layer(group, normed, hidden, topk_idx[0, 0], chunk_len, w_router, w_sh_gate, w_sh_up, w_sh_down, w_exp_gate, w_exp_up, w_exp_down)
+        return result.reshape(x_in.shape), lat_upd.reshape(lat_cache.shape), rope_upd.reshape(rope_cache.shape)
 
     return jax.shard_map(device_step, mesh=mesh, in_specs=(tok_spec,) * 6 + (whole,) * 13 + (exp_spec,) * 3, out_specs=(tok_spec, tok_spec, tok_spec), check_vma=False)

time: 519 us -> 440 us (0.85)
  the two profiles are of different devices: /device:TPU:151 before, /device:TPU:21 now
where the time goes in v2:
time: 440 us
  Pallas kernels  430 us (98%)
  local copies, waits for them, and re-layouts  6.1 us (1%)
    pallas_call x1, Pallas kernels, moe_layer(): pl.pallas_call(functools.partial(moe_kernel, dims), out_shape=[jax.ShapeD...  378 us
    pallas_call x1, Pallas kernels, attention_block(): pl.pallas_call(functools.partial(attn_kernel, qdim ** (-0.5)), out_shape=...  52.5 us

profile of v2, /device:TPU:21, one launch (start us, length us, event | category | flops | bytes accessed | tf_op | source)
XLA Modules:
  0.0 439.8 jit_solution(18422447849660672110)
XLA Ops:
  1.9 0.7 concatenate.24
  2.6 0.7 concatenate.22
  3.3 0.7 concatenate.23
  4.0 0.6 maximum_convert_fusion.gains_ref
  4.6 0.7 copy.27
  5.3 0.6 concatenate.27.tk_ref
  5.9 0.3 multiply_cosine_fusion
  6.2 0.6 maximum_bitcast_fusion.tab_ref
  6.8 52.5 %shard_map.229 = (bf16[384,2048]{1,0:T(8,128)(2,1)}, bf16[384,2048]{1,0:T(8,128)(2,1)}, bf16[1024,512]{1,0:T(8,128)(2,1)}, bf16[64,1024]{1,0:T(8,128)(2,1)}) custom-call(s32[1]{0:T(128)} %bitcast.28.len_ref, s32[1]{0:T(128)} %bitcast.31.ctx_ref, bf16[384,2048]{1,0:T(8,128)(2,1)} %bitcast.38, f32[1,4608]{1,0:T(1,128)} %maximum_convert_fusion.gains_ref, ...), custom_call_target="tpu_custom_call" | custom-call | tf_op jit(solution)/shard_map/pallas_call | solution.py:151
  59.3 377.8 %shard_map.230 = (bf16[384,2048]{1,0:T(8,128)(2,1)}, bf16[16,384,2048]{2,1,0:T(8,128)(2,1)}) custom-call(bf16[384,2048]{1,0:T(8,128)(2,1)} %get-tuple-element.8.u_ref, bf16[384,2048]{1,0:T(8,128)(2,1)} %get-tuple-element.9.h_ref, s32[8,384]{1,0:T(8,128)} %concatenate.27.tk_ref, s32[1]{0:T(128)} %bitcast.29.len_ref, bf16[64,2048]{1,0:T(8,128)(2,1)} %bitcast.42, ...), custom_call_target="tpu_custom_call" | custom-call | tf_op jit(solution)/shard_map/pallas_call | solution.py:587
  437.1 2.7 copy.31
  (2 shorter events, 0.0 us)

commit v3 on v2

--- a/solution.py
+++ b/solution.py
@@ -28,7 +28,7 @@
     return jnp.cos(angle), jnp.sin(angle)
 
 
-def attn_kernel(scale, len_ref, ctx_ref, x_hbm, gains_ref, tab_ref, dkv_hbm, kr_hbm, q_hbm, lat_hbm, rope_hbm, uk_hbm, uv_hbm, wo_hbm, h_ref, u_ref, lat_ref, rope_ref, x, dkv, kr, q, lat_old, rope_old, uk, uv, wo, uk_wide, uv_wide, turned, lat_t, rope_rows, heads_out, sems, q_sems):
+def attn_kernel(scale, len_ref, ctx_ref, x_hbm, gattn_ref, gffn_ref, gkv_ref, tab_ref, dkv_hbm, kr_hbm, q_hbm, lat_hbm, rope_hbm, uk_hbm, uv_hbm, wo_hbm, h_ref, u_ref, lat_ref, rope_ref, x, dkv, kr, q, lat_old, rope_old, uk, uv, wo, uk_wide, uv_wide, turned, lat_t, rope_rows, heads_out, sems, q_sems):
     heads, qdim, width = q.shape
     ctx_max, rank = lat_old.shape
     rope_dim = rope_old.shape[0]
@@ -60,14 +60,15 @@
         second = vals[half:]
         return jnp.concatenate([first * cos_tab - second * sin_tab, second * cos_tab + first * sin_tab], axis=0).astype(BF16)
 
-    def normed(vals, gain):
+    def normed(vals, gain_ref):
+        gain = gain_ref[...].astype(F32).reshape(1, gain_ref.shape[0])
         return vals * lax.rsqrt(jnp.mean(vals * vals, axis=1, keepdims=True) + EPS) * gain
 
     copies[0].wait()
-    a = normed(x[...].astype(F32), gains_ref[:, :width]).astype(BF16)
+    a = normed(x[...].astype(F32), gattn_ref).astype(BF16)
     turned[...] = jnp.transpose(a.astype(F32)).astype(BF16)
     copies[1].wait()
-    lat_new = normed(jnp.dot(a, dkv[...], preferred_element_type=F32), gains_ref[:, 2 * width:]).astype(BF16)
+    lat_new = normed(jnp.dot(a, dkv[...], preferred_element_type=F32), gkv_ref).astype(BF16)
     copies[2].wait()
     rope_new = roped(jnp.dot(kr[...], turned[...], preferred_element_type=F32))
     place = lax.broadcasted_iota(jnp.int32, (ctx_max, chunk), 0) - ctx
@@ -130,7 +131,8 @@
 
     total = lax.fori_loop(0, width // 256, project, jnp.zeros((chunk, 1), F32))
     inv = lax.rsqrt(total / width + EPS)
-    u_ref[...] = (h_ref[...].astype(F32) * inv * gains_ref[:, width:2 * width]).astype(BF16)
+    gain = gffn_ref[...].astype(F32).reshape(1, width)
+    u_ref[...] = (h_ref[...].astype(F32) * inv * gain).astype(BF16)
 
 
 def attention_block(x, chunk_len, ctx_len, lat_cache, rope_cache, g_attn, w_q, w_dkv, g_kv, w_kr, w_uk, w_uv, w_o, g_ffn):
@@ -141,7 +143,6 @@
     nope = qdim - rope_dim
     vdim = w_uv.shape[2]
     tab = jnp.concatenate(rope_tables(ctx_len.reshape(1) + jnp.arange(chunk), rope_dim // 2), axis=1).T
-    gains = jnp.concatenate([g_attn, g_ffn, g_kv]).astype(F32).reshape(1, 2 * width + rank)
     vmem = pl.BlockSpec(memory_space=pltpu.VMEM)
     hbm = pl.BlockSpec(memory_space=pl.ANY)
     smem = pl.BlockSpec(memory_space=pltpu.SMEM)
@@ -151,11 +152,11 @@
     hidden, normed, lat, rope = pl.pallas_call(
         functools.partial(attn_kernel, qdim ** -0.5),
         out_shape=[jax.ShapeDtypeStruct((chunk, width), BF16), jax.ShapeDtypeStruct((chunk, width), BF16), jax.ShapeDtypeStruct((ctx_max, rank), BF16), jax.ShapeDtypeStruct((rope_dim, ctx_max), BF16)],
-        in_specs=[smem, smem, hbm, vmem, vmem] + [hbm] * 8,
+        in_specs=[smem, smem, hbm, vmem, vmem, vmem, vmem] + [hbm] * 8,
         out_specs=[vmem] * 4,
         scratch_shapes=[pltpu.VMEM(shape, BF16) for shape in low] + [pltpu.VMEM(shape, F32) for shape in wide] + [pltpu.VMEM(shape, BF16) for shape in more] + [pltpu.SemaphoreType.DMA((8,)), pltpu.SemaphoreType.DMA((heads // 2,))],
         compiler_params=pltpu.CompilerParams(vmem_limit_bytes=67043328),
-    )(chunk_len.reshape(1), ctx_len.reshape(1), x, gains, tab, w_dkv, w_kr.T, w_q.transpose(1, 2, 0), lat_cache, rope_cache.T, w_uk.reshape(rank * heads, nope), w_uv.reshape(rank * heads, vdim), w_o.reshape(heads * vdim, width))
+    )(chunk_len.reshape(1), ctx_len.reshape(1), x, g_attn, g_ffn, g_kv, tab, w_dkv, w_kr.T, w_q.transpose(1, 2, 0), lat_cache, rope_cache.T, w_uk.reshape(rank * heads, nope), w_uv.reshape(rank * heads, vdim), w_o.reshape(heads * vdim, width))
     return hidden, normed, lat, rope.T
 
 
@@ -416,7 +417,7 @@
 
         lax.fori_loop(0, 4, gather, 0)
 
-        @pl.when(jnp.logical_and(c > 0, c < 3))
+        @pl.when(c == 2)
         def _():
             for j in range(4):
                 send_back(c - 1, j, source(c - 1, jnp.int32(j))).start()
@@ -439,6 +440,11 @@
                 @pl.when(jnp.logical_and(c == when_c, t == when_t * gu_tiles // 44))
                 def _():
                     relay(hop, part)
+
+            @pl.when(jnp.logical_and(c == 1, t == SEND_FIRST * gu_tiles // 44))
+            def _():
+                for j in range(4):
+                    send_back(c - 1, j, source(c - 1, jnp.int32(j))).start()
 
             @pl.when(jnp.logical_and(c == 3, t == HAND_ON * gu_tiles // 44))
             def _():
@@ -486,18 +492,19 @@
         return carry
 
     lax.fori_loop(0, 4, chunk, 0)
-    for j in range(4):
+    for j in (0, 1, 3, 2):
         send_back(jnp.int32(3), jnp.int32(j), source(jnp.int32(3), jnp.int32(j))).start()
 
     def combine(i, carry):
         c = lax.div(i, 4)
-        side = lax.rem(lax.div(i, 2), 2)
+        side = lax.rem(lax.div(i, 2) + core * lax.div(c, 3), 2)
+        at = 4 * c + 2 * side + lax.rem(i, 2)
         zz = zpos - (1 - side) * distance(c) + side * lax.rem(distance(c), far)
         who = dev(zz, lax.rem(i, 2))
 
-        @pl.when(i != 10 + core)
+        @pl.when(at != 10 + core)
         def _():
-            remote(sent.at[0, pl.ds(0, cap)], back.at[who], back_s.at[0], back_r.at[i], dev(zpos, 1 - core)).wait_recv()
+            remote(sent.at[0, pl.ds(0, cap)], back.at[who], back_s.at[0], back_r.at[at], dev(zpos, 1 - core)).wait_recv()
 
         mix = jnp.zeros((cap, tokens), F32)
         for k in range(top_k):
@@ -540,8 +547,9 @@
     to_sibling().wait_send()
 
 
-EVENTS = ((0, 16, 2, 0), (0, 40, 2, 1), (1, 4, 3, 0), (1, 24, 3, 1), (1, 43, 4, 0), (1, 43, 4, 1))
-HAND_ON = 34
+EVENTS = ((0, 16, 2, 0), (0, 40, 2, 1), (1, 4, 3, 0), (1, 20, 3, 1), (1, 43, 4, 0), (1, 43, 4, 1))
+SEND_FIRST = 26
+HAND_ON = 40
 
 
 def moe_layer(group, u, h, topk, chunk_len, w_router, wsg, wsu, wsd, wg, wu, wd):

time: 440 us -> 424 us (0.964)
  Pallas kernels: 430 us -> 416 us
    pallas_call x1, Pallas kernels: 378 us -> 363 us  [moe_layer(): pl.pallas_call(functools.partial(moe_kernel, dims), out_shape=[jax.ShapeD...]
where the time goes in v3:
time: 424 us; the launch traced here: 422 us
  Pallas kernels  416 us (98%)
    pallas_call x1, Pallas kernels, moe_layer(): pl.pallas_call(functools.partial(moe_kernel, dims), out_shape=[jax.ShapeD...  363 us
    pallas_call x1, Pallas kernels, attention_block(): pl.pallas_call(functools.partial(attn_kernel, qdim ** (-0.5)), out_shape=...  52.8 us

profile of v3, /device:TPU:21, one launch (start us, length us, event | category | flops | bytes accessed | tf_op | source)
XLA Modules:
  0.0 422.4 jit_solution(9509985208149753308)
XLA Ops:
  1.9 0.7 copy.27
  2.7 0.6 concatenate.7.tk_ref
  3.3 0.3 multiply_cosine_fusion
  3.5 0.6 maximum_bitcast_fusion.tab_ref
  4.1 52.8 %shard_map.229 = (bf16[384,2048]{1,0:T(8,128)(2,1)}, bf16[384,2048]{1,0:T(8,128)(2,1)}, bf16[1024,512]{1,0:T(8,128)(2,1)}, bf16[64,1024]{1,0:T(8,128)(2,1)}) custom-call(s32[1]{0:T(128)} %bitcast.28.len_ref, s32[1]{0:T(128)} %bitcast.31.ctx_ref, bf16[384,2048]{1,0:T(8,128)(2,1)} %bitcast.38, bf16[2048]{0:T(1024)(128)(2,1)} %gattn_ref.1, ...), custom_call_target="tpu_custom_call" | custom-call | tf_op jit(solution)/shard_map/pallas_call | solution.py:152
  56.9 362.8 %shard_map.230 = (bf16[384,2048]{1,0:T(8,128)(2,1)}, bf16[16,384,2048]{2,1,0:T(8,128)(2,1)}) custom-call(bf16[384,2048]{1,0:T(8,128)(2,1)} %get-tuple-element.8.u_ref, bf16[384,2048]{1,0:T(8,128)(2,1)} %get-tuple-element.9.h_ref, s32[8,384]{1,0:T(8,128)} %concatenate.7.tk_ref, s32[1]{0:T(128)} %bitcast.29.len_ref, bf16[64,2048]{1,0:T(8,128)(2,1)} %bitcast.42, ...), custom_call_target="tpu_custom_call" | custom-call | tf_op jit(solution)/shard_map/pallas_call | solution.py:595
  419.7 2.7 copy.31
  (2 shorter events, 0.0 us)
